TPU v7x, 8 devices: a whole 2x2x1 slice. The times are simulated.
8 devices in a mesh: dp: 1 (over z), ep: 8 (over y, x, core).
Axes of the slice: x: 2, y: 2, z: 1, core: 2. Of those that a mesh axis runs over, the one named last changes fastest.
Arguments:
- hidden_in: bfloat16 [1536, 2048], P(('dp', 'ep'))
- norm_gain: float32 [2048], replicated
- router_w: float32 [64, 2048], replicated
- w_gate: bfloat16 [64, 2048, 1408], P('ep')
- w_up: bfloat16 [64, 2048, 1408], P('ep')
- w_down: bfloat16 [64, 1408, 2048], P('ep')
- ws_gate: bfloat16 [2048, 2816], replicated
- ws_up: bfloat16 [2048, 2816], replicated
- ws_down: bfloat16 [2816, 2048], replicated
- expert_ids: int32 [1536, 6], P(('dp', 'ep'))
Outputs:
- output: bfloat16 [1536, 2048], P(('dp', 'ep'))
All inputs are finite; a program needn't handle non-finite values.
Results may differ from a plain program's by a relative error of at most 0.00436671.
Values are sent between devices in bfloat16 or wider.
A program may use at most 1 GiB of HBM per device.

v0:
```python
import jax
import jax.numpy as jnp
from jax import lax
from jax.sharding import PartitionSpec as P

NORM_EPS = 1e-6
ROUTE_SCALE = 2.5
GROUPS = 8
GROUP_LIMIT = 4


def rms_norm(x_rows, norm_gain):
    x_f32 = x_rows.astype(jnp.float32)
    inv_rms = lax.rsqrt(jnp.mean(x_f32 * x_f32, axis=-1, keepdims=True) + NORM_EPS)
    return (x_f32 * inv_rms * norm_gain).astype(jnp.bfloat16)


def route_gates(x_norm, router_w, expert_ids):
    logits = jnp.einsum("td,nd->tn", x_norm.astype(jnp.float32), router_w, precision=lax.Precision.HIGHEST, preferred_element_type=jnp.float32)
    picked = jnp.take_along_axis(jax.nn.sigmoid(logits), expert_ids, axis=1)
    return ROUTE_SCALE * picked / jnp.sum(picked, axis=1, keepdims=True)


def swiglu(tok_rows, gate_mat, up_mat, down_mat):
    h_gate = jnp.dot(tok_rows, gate_mat, preferred_element_type=jnp.float32)
    h_up = jnp.dot(tok_rows, up_mat, preferred_element_type=jnp.float32)
    hidden = (jax.nn.silu(h_gate) * h_up).astype(jnp.bfloat16)
    return jnp.dot(hidden, down_mat, preferred_element_type=jnp.float32).astype(jnp.bfloat16)


def expert_stack(expert_in, w_gate, w_up, w_down):
    h_gate = jnp.einsum("ecd,edi->eci", expert_in, w_gate, preferred_element_type=jnp.float32)
    h_up = jnp.einsum("ecd,edi->eci", expert_in, w_up, preferred_element_type=jnp.float32)
    hidden = (jax.nn.silu(h_gate) * h_up).astype(jnp.bfloat16)
    return jnp.einsum("eci,eid->ecd", hidden, w_down, preferred_element_type=jnp.float32).astype(jnp.bfloat16)


def solution(mesh):
    ep_size = mesh.shape["ep"]

    def local_block(hidden_in, norm_gain, router_w, w_gate, w_up, w_down, ws_gate, ws_up, ws_down, expert_ids):
        tok_dev, top_k = expert_ids.shape
        model_dim = hidden_in.shape[1]
        exp_dev = w_gate.shape[0]
        pair_cap = GROUPS * ((top_k + GROUP_LIMIT - 1) // GROUP_LIMIT) * tok_dev // ep_size
        recv_cap = pair_cap * ep_size
        exp_cap = recv_cap // exp_dev
        x_norm = rms_norm(hidden_in, norm_gain)
        gate_vals = route_gates(x_norm, router_w, expert_ids)
        shared_out = swiglu(x_norm, ws_gate, ws_up, ws_down)

        flat_ids = expert_ids.reshape(-1)
        dest_dev = flat_ids // exp_dev
        dest_hot = (dest_dev[:, None] == jnp.arange(ep_size, dtype=jnp.int32)[None, :]).astype(jnp.int32)
        dest_rank = jnp.sum((jnp.cumsum(dest_hot, axis=0) - 1) * dest_hot, axis=1)
        send_slot = dest_dev * pair_cap + dest_rank
        pair_tok = jnp.arange(tok_dev * top_k, dtype=jnp.int32) // top_k
        slot_tok = jnp.full((recv_cap,), tok_dev, jnp.int32).at[send_slot].set(pair_tok)
        slot_exp = jnp.full((recv_cap,), -1, jnp.int32).at[send_slot].set(flat_ids % exp_dev)
        send_rows = jnp.take(x_norm, slot_tok, axis=0, mode="fill", fill_value=0)
        recv_rows = lax.all_to_all(send_rows, "ep", 0, 0, tiled=True)
        recv_exp = lax.all_to_all(slot_exp, "ep", 0, 0, tiled=True)

        exp_hot = (recv_exp[:, None] == jnp.arange(exp_dev, dtype=jnp.int32)[None, :]).astype(jnp.int32)
        exp_rank = jnp.sum((jnp.cumsum(exp_hot, axis=0) - 1) * exp_hot, axis=1)
        buf_slot = jnp.where(recv_exp >= 0, recv_exp * exp_cap + exp_rank, recv_cap)
        buf_row = jnp.full((recv_cap,), recv_cap, jnp.int32).at[buf_slot].set(jnp.arange(recv_cap, dtype=jnp.int32), mode="drop")
        expert_in = jnp.take(recv_rows, buf_row, axis=0, mode="fill", fill_value=0).reshape(exp_dev, exp_cap, model_dim)
        expert_out = expert_stack(expert_in, w_gate, w_up, w_down).reshape(recv_cap, model_dim)
        back_rows = jnp.take(expert_out, buf_slot, axis=0, mode="fill", fill_value=0)
        returned = lax.all_to_all(back_rows, "ep", 0, 0, tiled=True)

        pair_out = jnp.take(returned, send_slot, axis=0).reshape(tok_dev, top_k, model_dim)
        routed = jnp.sum(gate_vals[:, :, None] * pair_out.astype(jnp.float32), axis=1)
        return (hidden_in.astype(jnp.float32) + shared_out.astype(jnp.float32) + routed).astype(jnp.bfloat16)

    row_spec = P(("dp", "ep"), None)
    in_specs = (row_spec, P(), P(), P("ep"), P("ep"), P("ep"), P(), P(), P(), row_spec)
    return jax.shard_map(local_block, mesh=mesh, in_specs=in_specs, out_specs=row_spec, check_vma=False)
```

profile of v0, /device:TPU:0, one launch (start us, length us, event | category | flops | bytes accessed | tf_op | source)
XLA Modules:
  0.0 550.9 jit_solution(13559009106431927132)
XLA Ops:
  0.0 0.9 copy.36
  0.9 0.1 reshape.263
  1.0 0.1 reshape.262
  1.2 0.1 reshape.265
  1.3 2.3 reduce-window.14
  3.6 0.3 slice_reduce_fusion.1
  3.9 0.2 reduce-window.15
  4.1 0.1 add_bitcast_fusion.1
  4.2 0.6 copy-done.3
  4.9 7.0 %scatter_custom_fusion.1 = s32[3072]{0:T(1024)} fusion(s32[1152]{0:T(1024)S(1)} %fusion.36, s32[1152]{0:T(1024)S(1)} %get-tuple-element.6, s32[]{:T(128)} %constant.117.clone.1), kind=kCustom, calls=%fused_computation.100 | custom fusion | bytes 12292 | tf_op jit(solution)/shard_map/scatter | solution.py:59
  11.9 4.3 all-to-all-start.1
  16.2 6.5 %scatter_custom_fusion = s32[3072]{0:T(1024)S(1)} fusion(s32[1152]{0:T(1024)S(1)} %fusion.36, s32[1152]{0:T(1024)S(1)} %add_select_fusion.1, s32[]{:T(128)} %constant.121.clone.1), kind=kCustom, calls=%fused_computation.104 | custom fusion | bytes 12292 | tf_op jit(solution)/shard_map/scatter | solution.py:58
  22.7 1.4 fusion.5
  24.1 1.4 fusion.7
  25.5 16.0 %gather_fusion = bf16[3072,2048]{1,0:T(8,128)(2,1)} fusion(bf16[192,2048]{1,0:T(8,128)(2,1)S(1)} %fusion.7, s32[3072]{0:T(1024)S(1)} %fusion.17), kind=kCustom, calls=%fused_computation.2 | custom fusion | bytes 25178112 | tf_op jit(solution)/shard_map/jit(_take)/gather | solution.py:60
  41.5 10.7 %broadcast_select_fusion.2 = bf16[8,384,2048]{2,1,0:T(8,128)(2,1)} fusion(bf16[8,384,2048]{2,1,0:T(8,128)(2,1)} %bitcast.74, pred[8,384]{1,0:T(8,128)(4,1)S(1)} %broadcast_in_dim.59), kind=kLoop, calls=%fused_computation.12 | loop fusion | flops 6291456 | bytes 25168896 | tf_op jit(solution)/shard_map/jit(_take)/select_n | solution.py:60
  52.2 0.0 all-to-all-done.1
  52.2 4.1 all-to-all-start
  56.3 2.3 reduce-window.16
  58.6 0.3 slice_reduce_fusion
  58.9 0.2 reduce-window.19
  59.1 0.1 add_bitcast_fusion
  59.3 11.8 %scatter_custom_fusion.2 = s32[3072]{0:T(1024)S(1)} fusion(s32[3072]{0:T(1024)S(1)} %bitcast.86, s32[3072]{0:T(1024)S(1)} %iota.21, s32[]{:T(128)} %constant.119.clone.1), kind=kCustom, calls=%fused_computation.102 | custom fusion | bytes 12292 | tf_op jit(solution)/shard_map/scatter | solution.py:67
  71.2 0.6 compare_and_fusion
  71.8 123.5 %all-to-all-done = bf16[8,384,2048]{2,1,0:T(8,128)(2,1)} async-done(((bf16[8,384,2048]{2,1,0:T(8,128)(2,1)}), bf16[8,384,2048]{2,1,0:T(8,128)(2,1)}, u32[]{:S(2)}, u32[]{:S(2)}) %all-to-all-start) | async-done | bytes 12582944 | tf_op jit(solution)/shard_map/all_to_all | solution.py:61
  195.2 30.2 %gather_fusion.3 = bf16[3072,2048]{1,0:T(8,128)(2,1)} fusion(bf16[3072,2048]{1,0:T(8,128)(2,1)} %bitcast.11, s32[3072]{0:T(1024)S(1)} %fusion.18), kind=kCustom, calls=%fused_computation.clone | custom fusion | bytes 25178112 | tf_op jit(solution)/shard_map/jit(_take)/gather | solution.py:68
  225.5 11.0 %broadcast_select_fusion.1 = bf16[3072,2048]{1,0:T(8,128)(2,1)} fusion(bf16[3072,2048]{1,0:T(8,128)(2,1)} %gather_fusion.3, pred[3072]{0:T(1024)(128)(4,1)S(1)} %compare_and_fusion.1), kind=kLoop, calls=%fused_computation.11 | loop fusion | flops 6291456 | bytes 25168896 | tf_op jit(solution)/shard_map/jit(_take)/select_n | solution.py:68
  236.5 32.1 %fusion.44 = f32[8,384,1408]{2,1,0:T(8,128)} fusion(bf16[8,384,2048]{2,1,0:T(8,128)(2,1)} %bitcast.75, bf16[8,2048,1408]{2,1,0:T(8,128)(2,1)} %param.15), kind=kOutput, calls=%fused_computation.112 | convolution fusion | flops 17716740096 | bytes 76021760 | tf_op jit(solution)/shard_map/ecd,edi->eci/dot_general | solution.py:32
  268.6 50.3 %convolution_convert_fusion = bf16[8,384,2048]{2,1,0:T(8,128)(2,1)} fusion(bf16[8,1408,2048]{2,1,0:T(8,128)(2,1)} %param.17, f32[8,384,1408]{2,1,0:T(8,128)} %fusion.44, bf16[8,384,2048]{2,1,0:T(8,128)(2,1)} %bitcast.76, bf16[8,2048,1408]{2,1,0:T(8,128)(2,1)} %param.16), kind=kOutput, calls=%fused_computation.13 | convolution fusion | flops 35465723904 | bytes 134742016 | tf_op jit(solution)/shard_map/eci,eid->ecd/dot_general | solution.py:35
  318.9 30.0 %gather_fusion.4 = bf16[3072,2048]{1,0:T(8,128)(2,1)} fusion(bf16[3072,2048]{1,0:T(8,128)(2,1)} %bitcast.72, s32[3072]{0:T(1024)S(1)} %broadcast_clamp_fusion), kind=kCustom, calls=%fused_computation.1.clone | custom fusion | bytes 25178112 | tf_op jit(solution)/shard_map/jit(_take)/gather | solution.py:70
  348.9 11.0 %broadcast_select_fusion = bf16[3072,2048]{1,0:T(8,128)(2,1)} fusion(bf16[3072,2048]{1,0:T(8,128)(2,1)} %gather_fusion.4, pred[3072]{0:T(1024)(128)(4,1)S(1)} %copy-done.7), kind=kLoop, calls=%fused_computation.10 | loop fusion | flops 6291456 | bytes 25168896 | tf_op jit(solution)/shard_map/jit(_take)/select_n | solution.py:70
  360.0 4.4 all-to-all-start.2
  364.4 0.1 reduce_sum.54
  364.6 0.1 copy.38
  364.7 0.2 copy.39
  364.9 0.1 copy.33
  365.0 0.1 reshape.301
  365.2 1.0 fusion.10
  366.2 9.3 %gather_fusion.2 = f32[1152]{0:T(1024)S(1)} fusion(f32[192,64]{0,1:T(8,128)S(1)} %fusion.10, s32[1152]{0:T(1024)S(1)} %reshape.301), kind=kCustom, calls=%fused_computation.4 | custom fusion | bytes 18432 | tf_op jit(solution)/shard_map/jit(take_along_axis)/gather | solution.py:20
  375.5 0.1 reshape.304
  375.6 0.1 copy.34
  375.7 0.1 copy.35
  375.9 8.1 %fusion.42 = f32[192,2816]{1,0:T(8,128)} fusion(bf16[2048,2816]{1,0:T(8,128)(2,1)} %param.18, bf16[192,2048]{1,0:T(8,128)(2,1)S(1)} %copy-done.1, f32[2048]{0:T(1024)S(1)} %copy-done.8, f32[192]{0:T(256)S(1)} %copy-done.10), kind=kOutput, calls=%fused_computation.111 | convolution fusion | flops 2216165376 | bytes 14492416 | tf_op jit(solution)/shard_map/dot_general | solution.py:25
  384.0 119.2 %all-to-all-done.2 = bf16[8,384,2048]{2,1,0:T(8,128)(2,1)} async-done(((bf16[8,384,2048]{2,1,0:T(8,128)(2,1)}), bf16[8,384,2048]{2,1,0:T(8,128)(2,1)}, u32[]{:S(2)}, u32[]{:S(2)}) %all-to-all-start.2) | async-done | bytes 12582944 | tf_op jit(solution)/shard_map/all_to_all | solution.py:71
  503.2 16.8 %gather_fusion.1 = bf16[1152,2048]{1,0:T(8,128)(2,1)} fusion(bf16[3072,2048]{1,0:T(8,128)(2,1)} %bitcast.15, s32[2048]{0:T(1024)S(1)} %pad_clamp_fusion), kind=kCustom, calls=%fused_computation.3 | custom fusion | bytes 9441792 | tf_op jit(solution)/shard_map/jit(_take)/gather | solution.py:73
  520.0 8.4 %gather.23 = bf16[192,6,2048]{2,1,0:T(8,128)(2,1)} reshape(bf16[1152,2048]{1,0:T(8,128)(2,1)} %gather_fusion.1) | data formatting | bytes 9437184 | tf_op jit(solution)/shard_map/jit(_take)/gather | solution.py:73
  528.4 8.5 %multiply_reduce_fusion = f32[192,2048]{1,0:T(8,128)S(1)} fusion(bf16[192,6,2048]{2,1,0:T(8,128)(2,1)} %gather.23, f32[192,6]{1,0:T(8,128)S(1)} %copy.35, pred[192,6]{1,0:T(8,128)(4,1)S(1)} %copy.39), kind=kLoop, calls=%fused_computation.9 | loop fusion | flops 9043968 | bytes 6297216 | tf_op jit(solution)/shard_map/reduce_sum | solution.py:74
  537.0 13.9 %fusion.4 = bf16[192,2048]{1,0:T(8,128)(2,1)} fusion(f32[192,2048]{1,0:T(8,128)S(1)} %multiply_reduce_fusion, bf16[2816,2048]{1,0:T(8,128)(2,1)} %param.20, bf16[192,2048]{1,0:T(8,128)(2,1)S(1)} %copy-done.1, bf16[2048,2816]{1,0:T(8,128)(2,1)} %param.19, f32[192,2816]{1,0:T(8,128)} %fusion.42, f32[2048]{0:T(1024)S(1)} %copy-done.8, f32[192]{0:T(256)S(1)} %copy-done.10), kind=kOutput, calls=%fused_computation.20 | convolution fusion | flops 4436361216 | bytes 28386048 | tf_op jit(solution)/shard_map/dot_general | solution.py:28
  (45 shorter events, 0.4 us)
Async XLA Ops:
  0.0 365.1 %copy-start = (f32[64,2048]{1,0:T(8,128)S(1)}, f32[64,2048]{1,0:T(8,128)}, u32[]{:S(2)}) copy-start(f32[64,2048]{1,0:T(8,128)} %param.14) | copy-start | bytes 1572868
  4.2 0.6 copy-start.3
  4.9 19.2 %copy-start.5 = (s32[1152]{0:T(1024)}, s32[1152]{0:T(1024)S(1)}, u32[]{:S(2)}) copy-start(s32[1152]{0:T(1024)S(1)} %fusion.36) | copy-start | bytes 13828
  11.9 40.3 %all-to-all-start.1 = ((s32[8,384,1]{1,2,0:T(1,128)}), s32[8,384,1]{1,2,0:T(1,128)S(1)}, u32[]{:S(2)}, u32[]{:S(2)}) async-start(s32[8,384,1]{1,2,0:T(1,128)} %bitcast.2), calls=%async_computation.1 | async-start | bytes 24576 | tf_op jit(solution)/shard_map/all_to_all | solution.py:62
  24.1 17.4 %copy-start.9 = (f32[192]{0:T(256)}, f32[192]{0:T(256)S(1)}, u32[]{:S(2)}) copy-start(f32[192]{0:T(256)S(1)} %add_rsqrt_fusion) | copy-start | bytes 2308
  52.2 143.1 %all-to-all-start = ((bf16[8,384,2048]{2,1,0:T(8,128)(2,1)}), bf16[8,384,2048]{2,1,0:T(8,128)(2,1)}, u32[]{:S(2)}, u32[]{:S(2)}) async-start(bf16[8,384,2048]{2,1,0:T(8,128)(2,1)} %broadcast_select_fusion.2), calls=%async_computation | async-start | bytes 25165824 | tf_op jit(solution)/shard_map/all_to_all | solution.py:61
  318.9 30.0 %copy-start.7 = (pred[3072]{0:T(1024)(128)(4,1)S(1)}, pred[3072]{0:T(1024)(128)(4,1)}, u32[]{:S(2)}) copy-start(pred[3072]{0:T(1024)(128)(4,1)} %compare_and_fusion) | copy-start | bytes 9220
  359.9 4.5 copy-start.4
  359.9 4.7 copy-start.2
  359.9 5.2 copy-start.1
  360.0 5.2 copy-start.8
  360.0 5.2 copy-start.10
  360.0 143.2 %all-to-all-start.2 = ((bf16[8,384,2048]{2,1,0:T(8,128)(2,1)}), bf16[8,384,2048]{2,1,0:T(8,128)(2,1)}, u32[]{:S(2)}, u32[]{:S(2)}) async-start(bf16[8,384,2048]{2,1,0:T(8,128)(2,1)} %bitcast.73), calls=%async_computation.2 | async-start | bytes 25165824 | tf_op jit(solution)/shard_map/all_to_all | solution.py:71
  366.1 9.7 %copy-start.6 = (s32[1152]{0:T(1024)S(1)}, s32[1152]{0:T(1024)}, u32[]{:S(2)}) copy-start(s32[1152]{0:T(1024)} %copy-done.5) | copy-start | bytes 13828
where the time goes:
time: 552 us; the launch traced here: 551 us
  waiting for transfers between devices  243 us (44%)
  local copies, waits for them, and re-layouts  140 us (25%)
  matrix products  105 us (19%)
  other arithmetic  50.1 us (9%)
  starting transfers between devices  12.8 us (2%)
    all_to_all x1, waiting for transfers between devices, local_block(): recv_rows = lax.all_to_all(send_rows, 'ep', 0, 0, tiled=True)  123 us
    all_to_all x1, waiting for transfers between devices, local_block(): returned = lax.all_to_all(back_rows, 'ep', 0, 0, tiled=True)  119 us
    dot_general x1, matrix products, expert_stack(): jnp.einsum('eci,eid->ecd', hidden, w_down, preferred_element_type=jnp.flo...  50.3 us
    dot_general x1, matrix products, expert_stack(): jnp.einsum('ecd,edi->eci', expert_in, w_gate, preferred_element_type=jnp....  32.1 us
    gather x1, local copies, waits for them, and re-layouts, local_block(): jnp.take(recv_rows, buf_row, axis=0, mode='fill', fill_value=0)  30.2 us
    gather x1, local copies, waits for them, and re-layouts, local_block(): jnp.take(expert_out, buf_slot, axis=0, mode='fill', fill_value=0)  30 us
    gather x2, local copies, waits for them, and re-layouts, local_block(): jnp.take(returned, send_slot, axis=0).reshape(tok_dev, top_k, model_dim)  25.3 us
    gather x1, local copies, waits for them, and re-layouts, local_block(): send_rows = jnp.take(x_norm, slot_tok, axis=0, mode='fill', fill_value=0)  16 us
  transfers between devices with their start and end apart: 3, of which 2 were waited for; matrix products, arithmetic and copies ran while one was open for 13% of the time, Pallas kernels for 0%

commit v1 on v0

v1 whole, which is shorter than its diff:
```python
import functools

import jax
import jax.numpy as jnp
from jax import lax
from jax.experimental import pallas as pl
from jax.experimental.pallas import tpu as pltpu
from jax.sharding import PartitionSpec as P

NORM_EPS = 1e-6
ROUTE_SCALE = 2.5
GROUPS = 8
GROUP_LIMIT = 4
F32 = jnp.float32
BF16 = jnp.bfloat16
VMEM_LIMIT = 67_000_000


def dot_f32(a, b):
    return jnp.dot(a, b, preferred_element_type=F32)


def place():
    me = lax.axis_index("ep")
    core = lax.rem(me, 2)
    x = lax.rem(me // 2, 2)
    y = me // 4
    return me, core, x, y, me + 1 - 2 * core, me + 2 - 4 * x, me + 4 - 8 * y


def pos_of(dev):
    return lax.rem(dev, 2) * 4 + dev // 2


def rcopy(src, dst, ssem, rsem, dev):
    return pltpu.make_async_remote_copy(
        src_ref=src, dst_ref=dst, send_sem=ssem, recv_sem=rsem, device_id={"ep": dev}, device_id_type=pl.DeviceIdType.MESH
    )


def gather_up_kernel(
    n_kc, cap, hid_ref, gain_ref, rw_ref, ids_ref, wg_ref, wu_ref, h_ref, rg_ref, xn_ref,
    xall, onehot, acc, wbuf, hbuf, xe, rank_s, meta_s, meta_r, w_sem, h_sem, m_send, m_recv, a_send, a_recv,
):
    me, core, x, y, sib, xnb, ynb = place()
    tok, dim = hid_ref.shape
    n_exp, _, inter = wg_ref.shape
    kw = dim // n_kc
    half = tok // 2
    grp = acc.shape[0]
    n_steps = n_exp * n_kc
    slots = wbuf.shape[0]

    def step_of(s):
        g = s // (grp * n_kc)
        r = lax.rem(s, grp * n_kc)
        return g * grp + lax.rem(r, grp), lax.rem(r, grp), r // grp

    def w_copies(s):
        e, _, kc = step_of(s)
        slot = lax.rem(s, slots)
        rows = pl.ds(pl.multiple_of(kc * kw, kw), kw)
        return (
            pltpu.make_async_copy(wg_ref.at[e, rows, :], wbuf.at[slot, :, pl.ds(0, inter)], w_sem.at[slot, 0]),
            pltpu.make_async_copy(wu_ref.at[e, rows, :], wbuf.at[slot, :, pl.ds(inter, inter)], w_sem.at[slot, 1]),
        )

    def w_start(s):
        for c in w_copies(s):
            c.start()

    for s in range(slots - 1):
        w_start(jnp.int32(s))

    barrier = pltpu.get_barrier_semaphore()
    for k in range(1, 8):
        pl.semaphore_signal(barrier, inc=1, device_id={"ep": lax.rem(me + k, 8)}, device_id_type=pl.DeviceIdType.MESH)

    x_f32 = hid_ref[...].astype(F32)
    inv_rms = lax.rsqrt(jnp.mean(x_f32 * x_f32, axis=-1, keepdims=True) + NORM_EPS)
    x_norm = (x_f32 * inv_rms * gain_ref[...]).astype(BF16)
    xn_ref[...] = x_norm
    my_pos = pos_of(me)
    my_rows = pl.ds(pl.multiple_of(my_pos * tok, tok), tok)
    for kc in range(n_kc):
        xall[kc, my_rows, :] = x_norm[:, kc * kw : (kc + 1) * kw]

    pl.semaphore_wait(barrier, 7)

    def block(kc, dev, part=None):
        start = pos_of(dev) * tok + (0 if part is None else part * half)
        n = tok if part is None else half
        return xall.at[kc, pl.ds(pl.multiple_of(start, half), n), :]

    def send(kc, kind, dev_src, to, part=None):
        ref = block(kc, dev_src, part)
        return rcopy(ref, ref, a_send.at[kc, kind], a_recv.at[kc, kind], to)

    diag = me + 6 - 4 * x - 8 * y
    kinds = (
        (me, sib, None), (me, xnb, None), (me, ynb, None), (xnb, ynb, 0), (ynb, xnb, 1),
        (xnb, sib, None), (ynb, sib, None), (diag, sib, 0), (diag, sib, 1),
    )

    def copy(kc, kind):
        src, to, part = kinds[kind]
        return send(kc, kind, src, to, part)

    def start(kc, which):
        for kind in which:
            copy(kc, kind).start()

    def received(kc, which):
        for kind in which:
            copy(kc, kind).wait_recv()

    def serve_a(kc):
        received(kc, (1, 2))
        start(kc, (3, 4, 5, 6))
        if kc + 1 < n_kc:
            start(kc + 1, (1, 2, 0))

    def serve_b(kc):
        received(kc, (3, 4))
        start(kc, (7, 8))

    def arrived(kc):
        received(kc, (0, 5, 6, 7, 8))

    start(0, (1, 2, 0))

    logits = lax.dot_general(
        rw_ref[...], x_norm.astype(F32), (((1,), (1,)), ((), ())), precision=lax.Precision.HIGHEST, preferred_element_type=F32
    )
    scores = jax.nn.sigmoid(logits)
    exp_iota = lax.broadcasted_iota(jnp.int32, scores.shape, 0)
    chosen = exp_iota == ids_ref[0:1, :tok]
    for j in range(1, 6):
        chosen = chosen | (exp_iota == ids_ref[j : j + 1, :tok])
    picked = jnp.where(chosen, scores, 0.0)
    gates = ROUTE_SCALE * picked / jnp.sum(picked, axis=0, keepdims=True)
    gates = jnp.where(chosen, gates, -1.0)
    meta_s[...] = jnp.full(meta_s.shape, -1.0, F32)
    for d in range(8):
        meta_s[d, :, 0:tok] = gates[d * n_exp : (d + 1) * n_exp, :]
    meta_r[pl.ds(my_pos, 1)] = meta_s[pl.ds(me, 1)]

    def meta(k):
        to = lax.rem(me + k, 8)
        return rcopy(meta_s.at[to], meta_r.at[my_pos], m_send.at[k], m_recv.at[k], to)

    for k in range(1, 8):
        meta(k).start()
    for k in range(1, 8):
        meta(k).wait_recv()

    lane = lax.broadcasted_iota(jnp.int32, (n_exp, 128), 1)
    tiles = []
    for m in range(4):
        a = meta_r[2 * m]
        b = pltpu.roll(meta_r[2 * m + 1], 64, 1)
        tiles += [a[:, :128], jnp.where(lane < 64, a[:, 128:], b[:, :128]), b[:, 128:]]
    masks = [t >= 0.0 for t in tiles]
    ones = jnp.concatenate([jnp.where(m, 1.0, 0.0) for m in masks], axis=0).astype(BF16)
    upper = lax.broadcasted_iota(jnp.int32, (128, 128), 0) <= lax.broadcasted_iota(jnp.int32, (128, 128), 1)
    counts = dot_f32(ones, jnp.where(upper, 1.0, 0.0).astype(BF16))
    before = jnp.zeros((n_exp, 1), F32)
    for i in range(12):
        cum = counts[i * n_exp : (i + 1) * n_exp]
        rank = jnp.where(masks[i], cum - 1.0 + before, -1.0)
        before = before + cum[:, 127:128]
        gate = jnp.where(masks[i], tiles[i], 0.0)
        for e in range(n_exp):
            rank_s[e, :, i * 128 : (i + 1) * 128] = rank[e : e + 1]
        packed = jnp.concatenate([rank, gate, jnp.zeros((128 - 2 * n_exp, 128), F32)], axis=0)
        rg_ref[i * 128 : (i + 1) * 128, :] = packed.T

    slot_iota = lax.broadcasted_iota(jnp.int32, (cap, 128), 0).astype(F32)

    def build(e, carry):
        for i in range(12):
            row = rank_s[e, :, i * 128 : (i + 1) * 128]
            onehot[e, :, i * 128 : (i + 1) * 128] = jnp.where(row == slot_iota, 1.0, 0.0).astype(BF16)
        return carry

    lax.fori_loop(0, n_exp, build, 0)

    serve_a(0)
    serve_b(0)
    arrived(0)

    def step(s, carry):
        e, el, kc = step_of(s)
        for c in range(1, n_kc):
            pl.when(s == grp * (c - 1) + 1)(functools.partial(serve_a, c))
            pl.when(s == grp * (c - 1) + grp - 1)(functools.partial(serve_b, c))
            pl.when(s == grp * c)(functools.partial(arrived, c))

        @pl.when(s + slots - 1 < n_steps)
        def _():
            w_start(s + slots - 1)

        for n in range(0, kw, 256):
            xe[:, n : n + 256] = dot_f32(onehot[e], xall[kc, :, n : n + 256]).astype(BF16)
        for c in w_copies(s):
            c.wait()
        slot = lax.rem(s, slots)
        for n in range(0, 2 * inter, 256):
            part = dot_f32(xe[...], wbuf[slot, :, n : n + 256])
            acc[el, :, n : n + 256] = jnp.where(kc > 0, acc[el, :, n : n + 256], 0.0) + part

        @pl.when(kc == n_kc - 1)
        def _():
            for n in range(0, inter, 128):
                g = acc[el, :, n : n + 128]
                u = acc[el, :, inter + n : inter + n + 128]
                hbuf[e, :, n : n + 128] = (jax.nn.silu(g) * u).astype(BF16)
            pltpu.make_async_copy(hbuf.at[e], h_ref.at[e], h_sem.at[e]).start()

        return carry

    lax.fori_loop(0, n_steps, step, 0)

    for e in range(n_exp):
        pltpu.make_async_copy(hbuf.at[e], h_ref.at[e], h_sem.at[e]).wait()
    for k in range(1, 8):
        meta(k).wait_send()
    for kc in range(n_kc):
        for kind in range(len(kinds)):
            copy(kc, kind).wait_send()


def down_kernel(
    n_chunk, hid_ref, xn_ref, rg_ref, h_ref, wd_ref, wsg_ref, wsu_ref, wsd_ref, out_ref,
    hv, place_t, gcol, wdb, part, got0, mid, got1, quart, got2, total, wsb, wdsb, hs,
    hv_sem, wd_sem, ws_sem, wds_sem, d_send, d_recv, p_send, p_recv, q_send, q_recv,
):
    me, core, x, y, sib, xnb, ynb = place()
    n_exp, cap, inter = h_ref.shape
    tok, dim = hid_ref.shape
    ctok = 4 * tok
    cw = dim // n_chunk
    hw = cw // 2
    unroll = 2
    per_chunk = n_exp // unroll
    n_steps = n_chunk * per_chunk
    slots = wdb.shape[0]

    def wd_copy(i):
        e, n, slot = lax.rem(i, n_exp), i // n_exp, lax.rem(i, slots)
        return pltpu.make_async_copy(wd_ref.at[e, :, pl.ds(pl.multiple_of(n * cw, cw), cw)], wdb.at[slot], wd_sem.at[slot])

    def h_copy(e):
        return pltpu.make_async_copy(h_ref.at[e], hv.at[e], hv_sem.at[e])

    h_copy(0).start()
    for i in range(slots - unroll):
        wd_copy(jnp.int32(i)).start()
    for e in range(1, n_exp):
        h_copy(e).start()

    barrier = pltpu.get_barrier_semaphore()
    for dev in (sib, xnb, ynb):
        pl.semaphore_signal(barrier, inc=1, device_id={"ep": dev}, device_id_type=pl.DeviceIdType.MESH)

    slot_iota = lax.broadcasted_iota(jnp.int32, (8 * tok, cap), 1).astype(F32)
    for e in range(n_exp):
        place_t[e] = jnp.where(rg_ref[:, e : e + 1] == slot_iota, 1.0, 0.0).astype(BF16)
        gcol[e] = jnp.broadcast_to(rg_ref[:, n_exp + e : n_exp + e + 1], (8 * tok, hw))
    pl.semaphore_wait(barrier, 3)

    def d_copy(n):
        b = lax.rem(n, 2)
        return rcopy(part.at[b, :, 1 - core], got0.at[b], d_send.at[b], d_recv.at[b], sib)

    def p_copies(n):
        b = lax.rem(n, 2)
        return (
            rcopy(mid.at[b, 0, :, 1 - x], got1.at[b, 0], p_send.at[b, 0], p_recv.at[b, 0], xnb),
            rcopy(mid.at[b, 1, 1 - y], got1.at[b, 1], p_send.at[b, 1], p_recv.at[b, 1], ynb),
        )

    def q_copies(n):
        b = lax.rem(n, 2)
        return (
            rcopy(quart.at[b, 0, 1 - y], got2.at[b, 0], q_send.at[b, 0], q_recv.at[b, 0], ynb),
            rcopy(quart.at[b, 1, 1 - x], got2.at[b, 1], q_send.at[b, 1], q_recv.at[b, 1], xnb),
        )

    def start(copies):
        for c in copies:
            c.start()

    def wait(copies):
        for c in copies:
            c.wait()

    def stage_p(n):
        b = lax.rem(n, 2)
        d_copy(n).wait()
        for hf in range(2):
            for yy in range(2):
                for xx in range(2):
                    rows = pl.ds((yy * 2 + xx) * tok, tok)
                    mid[b, hf, yy, xx] = part[b, hf, core, rows, :] + got0[b, hf, rows, :]
        start(p_copies(n))

    def stage_q(n):
        b = lax.rem(n, 2)
        wait(p_copies(n))
        for k in range(2):
            quart[b, 0, k] = mid[b, 0, k, x] + got1[b, 0, k]
            quart[b, 1, k] = mid[b, 1, y, k] + got1[b, 1, k]
        start(q_copies(n))

    def stage_f(n):
        b = lax.rem(n, 2)
        wait(q_copies(n))
        total[n, 0] = quart[b, 0, y] + got2[b, 0]
        total[n, 1] = quart[b, 1, x] + got2[b, 1]

    def step(s, carry):
        n, j = s // per_chunk, lax.rem(s, per_chunk)
        b = lax.rem(n, 2)

        for u in range(unroll):
            i = s * unroll + slots - unroll + u

            @pl.when(i < n_chunk * n_exp)
            def _():
                wd_copy(i).start()

        @pl.when(n == 0)
        def _():
            for u in range(unroll):
                h_copy(j * unroll + u).wait()

        for u in range(unroll):
            wd_copy(s * unroll + u).wait()

        outs = []
        for u in range(unroll):
            e = j * unroll + u
            slot = lax.rem(s * unroll + u, slots)
            outs.append(dot_f32(hv[e], wdb[slot]).astype(BF16))
        for half in range(2):
            rows = pl.ds(half * ctok, ctok)
            new = [dot_f32(place_t[j * unroll + u, rows, :], outs[u]) for u in range(unroll)]
            for hf in range(2):
                cols = slice(hf * hw, (hf + 1) * hw)
                val = jnp.where(j > 0, part[b, hf, half], 0.0)
                for u in range(unroll):
                    val = val + gcol[j * unroll + u, rows, :] * new[u][:, cols]
                part[b, hf, half] = val

        @pl.when(j == per_chunk // 2 - 1)
        def _():
            pl.when(n >= 3)(lambda: stage_f(n - 3))
            pl.when(n >= 2)(lambda: stage_q(n - 2))
            pl.when(n >= 1)(lambda: stage_p(n - 1))

        pl.when(j == per_chunk - 1)(lambda: d_copy(n).start())
        return carry

    lax.fori_loop(0, n_steps, step, 0)

    sw = wsb.shape[-1] // 2
    n_s = wsg_ref.shape[1] // sw

    def ws_copies(i):
        cols = pl.ds(pl.multiple_of(i * sw, sw), sw)
        slot = lax.rem(i, 2)
        return (
            pltpu.make_async_copy(wsg_ref.at[:, cols], wsb.at[slot, :, pl.ds(0, sw)], ws_sem.at[slot, 0]),
            pltpu.make_async_copy(wsu_ref.at[:, cols], wsb.at[slot, :, pl.ds(sw, sw)], ws_sem.at[slot, 1]),
        )

    last = jnp.int32(n_chunk - 1)
    start(ws_copies(jnp.int32(0)))
    stage_f(last - 2)
    stage_q(last - 1)
    stage_p(last)

    def shared_up(i, carry):
        @pl.when(i + 1 < n_s)
        def _():
            start(ws_copies(i + 1))

        wait(ws_copies(i))
        both = dot_f32(xn_ref[...], wsb[lax.rem(i, 2)])
        hs[i] = (jax.nn.silu(both[:, :sw]) * both[:, sw:]).astype(BF16)

        @pl.when(i == n_s // 2)
        def _():
            stage_f(last - 1)
            stage_q(last)

        return carry

    lax.fori_loop(0, n_s, shared_up, 0)

    dw = wdsb.shape[-1]
    n_d = dim // dw

    def wds_copy(i):
        slot = lax.rem(i, 2)
        return pltpu.make_async_copy(wsd_ref.at[:, pl.ds(pl.multiple_of(i * dw, dw), dw)], wdsb.at[slot], wds_sem.at[slot])

    wds_copy(jnp.int32(0)).start()
    stage_f(last)
    for i in range(n_d):
        if i + 1 < n_d:
            wds_copy(jnp.int32(i + 1)).start()
        wds_copy(jnp.int32(i)).wait()
        res = jnp.zeros((tok, dw), F32)
        for k in range(n_s):
            res = res + dot_f32(hs[k], wdsb[i % 2, k * sw : (k + 1) * sw, :])
        shared = res.astype(BF16).astype(F32)
        for c in range(0, dw, hw):
            col = i * dw + c
            routed = total[col // cw, (col % cw) // hw]
            cols = slice(col, col + hw)
            out_ref[:, cols] = (hid_ref[:, cols].astype(F32) + shared[:, c : c + hw] + routed).astype(BF16)


def solution(mesh):
    ep_size = mesh.shape["ep"]
    assert ep_size == 8

    def local_block(hidden_in, norm_gain, router_w, w_gate, w_up, w_down, ws_gate, ws_up, ws_down, expert_ids):
        tok, top_k = expert_ids.shape
        dim = hidden_in.shape[1]
        n_exp, _, inter = w_gate.shape
        s_inter = ws_gate.shape[1]
        cap = GROUPS * ((top_k + GROUP_LIMIT - 1) // GROUP_LIMIT) * tok // n_exp
        n_kc, grp, slots = 4, 4, 3
        vmem = pl.BlockSpec(memory_space=pltpu.VMEM)
        hbm = pl.BlockSpec(memory_space=pl.ANY)
        dma = pltpu.SemaphoreType.DMA
        ids_t = jnp.pad(expert_ids.T, ((0, 8 - top_k), (0, 256 - tok)), constant_values=-1)

        h, rg, xn = pl.pallas_call(
            functools.partial(gather_up_kernel, n_kc, cap),
            out_shape=(
                jax.ShapeDtypeStruct((n_exp, cap, inter), BF16),
                jax.ShapeDtypeStruct((8 * tok, 128), F32),
                jax.ShapeDtypeStruct((tok, dim), BF16),
            ),
            in_specs=[vmem, vmem, vmem, vmem, hbm, hbm],
            out_specs=(hbm, vmem, vmem),
            scratch_shapes=[
                pltpu.VMEM((n_kc, 8 * tok, dim // n_kc), BF16),
                pltpu.VMEM((n_exp, cap, 8 * tok), BF16),
                pltpu.VMEM((grp, cap, 2 * inter), F32),
                pltpu.VMEM((slots, dim // n_kc, 2 * inter), BF16),
                pltpu.VMEM((n_exp, cap, inter), BF16),
                pltpu.VMEM((cap, dim // n_kc), BF16),
                pltpu.VMEM((n_exp, 1, 8 * tok), F32),
                pltpu.VMEM((8, n_exp, 256), F32),
                pltpu.VMEM((8, n_exp, 256), F32),
                dma((slots, 2)),
                dma((n_exp,)),
                dma((8,)),
                dma((8,)),
                dma((n_kc, 9)),
                dma((n_kc, 9)),
            ],
            compiler_params=pltpu.CompilerParams(collective_id=0, has_side_effects=True, vmem_limit_bytes=VMEM_LIMIT),
            name="gather_up",
        )(hidden_in, norm_gain.reshape(1, dim), router_w, ids_t, w_gate, w_up)

        n_chunk, dslots = 8, 6
        cw = dim // n_chunk
        hw = cw // 2
        sw, dw = 256, 512
        return pl.pallas_call(
            functools.partial(down_kernel, n_chunk),
            out_shape=jax.ShapeDtypeStruct((tok, dim), BF16),
            in_specs=[vmem, vmem, vmem, hbm, hbm, hbm, hbm, hbm],
            out_specs=vmem,
            scratch_shapes=[
                pltpu.VMEM((n_exp, cap, inter), BF16),
                pltpu.VMEM((n_exp, 8 * tok, cap), BF16),
                pltpu.VMEM((n_exp, 8 * tok, hw), F32),
                pltpu.VMEM((dslots, inter, cw), BF16),
                pltpu.VMEM((2, 2, 2, 4 * tok, hw), F32),
                pltpu.VMEM((2, 2, 4 * tok, hw), F32),
                pltpu.VMEM((2, 2, 2, 2, tok, hw), F32),
                pltpu.VMEM((2, 2, 2, tok, hw), F32),
                pltpu.VMEM((2, 2, 2, tok, hw), F32),
                pltpu.VMEM((2, 2, tok, hw), F32),
                pltpu.VMEM((n_chunk, 2, tok, hw), F32),
                pltpu.VMEM((2, dim, 2 * sw), BF16),
                pltpu.VMEM((2, s_inter, dw), BF16),
                pltpu.VMEM((s_inter // sw, tok, sw), BF16),
                dma((n_exp,)),
                dma((dslots,)),
                dma((2, 2)),
                dma((2,)),
                dma((2,)),
                dma((2,)),
                dma((2, 2)),
                dma((2, 2)),
                dma((2, 2)),
                dma((2, 2)),
            ],
            compiler_params=pltpu.CompilerParams(collective_id=1, has_side_effects=True, vmem_limit_bytes=VMEM_LIMIT),
            name="down_sum",
        )(hidden_in, xn, rg, h, w_down, ws_gate, ws_up, ws_down)

    row_spec = P(("dp", "ep"), None)
    in_specs = (row_spec, P(), P(), P("ep"), P("ep"), P("ep"), P(), P(), P(), row_spec)
    return jax.shard_map(local_block, mesh=mesh, in_specs=in_specs, out_specs=row_spec, check_vma=False)
```

time: 552 us -> 194 us (0.35)
  waiting for transfers between devices: 243 us -> 0 us
  Pallas kernels: 0 us -> 190 us
  local copies, waits for them, and re-layouts: 140 us -> 3.39 us
  matrix products: 105 us -> 0 us
  other arithmetic: 50.1 us -> 0 us
  starting transfers between devices: 12.8 us -> 0 us
    all_to_all x3 -> x0, waiting for transfers between devices: 243 us -> none  [the longest x1 123 us: local_block(): recv_rows = lax.all_to_all(send_rows, 'ep', 0, 0, tiled=True)]
    pallas_call x0 -> x2, Pallas kernels: none -> 190 us  [the longest x1 103 us: local_block(): pl.pallas_call(functools.partial(gather_up_kernel, n_kc, cap), out_shape=...]
    gather x10 -> x0, local copies, waits for them, and re-layouts: 111 us -> none  [the longest x1 30.2 us: local_block(): jnp.take(recv_rows, buf_row, axis=0, mode='fill', fill_value=0)]
    dot_general x5 -> x0, matrix products: 105 us -> none  [the longest x1 50.3 us: expert_stack(): jnp.einsum('eci,eid->ecd', hidden, w_down, preferred_element_type=jnp.flo...]
    select_n x8 -> x0, other arithmetic: 32.9 us -> none  [the longest x1 11 us: local_block(): jnp.take(recv_rows, buf_row, axis=0, mode='fill', fill_value=0)]
    scatter x3 -> x0, local copies, waits for them, and re-layouts: 25.3 us -> none  [the longest x1 11.8 us: local_block(): jnp.full((recv_cap,), recv_cap, jnp.int32).at[buf_slot]]
    all_to_all x3 -> x0, starting transfers between devices: 12.8 us -> none  [the longest x1 4.44 us: local_block(): returned = lax.all_to_all(back_rows, 'ep', 0, 0, tiled=True)]
    reduce_sum x5 -> x0, other arithmetic: 9.98 us -> none  [the longest x1 8.5 us: local_block(): jnp.sum(gate_vals[:, :, None] * pair_out.astype(jnp.float32), axis=1)]
  transfers between devices with their start and end apart: 3 -> 0, of which waited for: 2 -> 0; matrix products, arithmetic and copies ran while one was open for 13% -> 0% of each run, Pallas kernels for 0% -> 0%
where the time goes in v1:
time: 194 us
  Pallas kernels  190 us (98%)
  local copies, waits for them, and re-layouts  3.39 us (2%)
    pallas_call x1, Pallas kernels, local_block(): pl.pallas_call(functools.partial(gather_up_kernel, n_kc, cap), out_shape=...  103 us
    pallas_call x1, Pallas kernels, local_block(): pl.pallas_call(functools.partial(down_kernel, n_chunk), out_shape=jax.Sha...  87.2 us

profile of v1, /device:TPU:0, one launch (start us, length us, event | category | flops | bytes accessed | tf_op | source)
XLA Modules:
  0.0 193.7 jit_solution(18392308968374978330)
XLA Ops:
  0.0 1.3 pad.4.ids_ref
  1.3 103.0 %gather_up.1 = (bf16[8,384,1408]{2,1,0:T(8,128)(2,1)}, f32[1536,128]{1,0:T(8,128)}, bf16[192,2048]{1,0:T(8,128)(2,1)}) custom-call(bf16[192,2048]{1,0:T(8,128)(2,1)} %hid_ref.3, f32[1,2048]{1,0:T(1,128)} %bitcast.2, f32[64,2048]{1,0:T(8,128)} %rw_ref.1, s32[8,256]{1,0:T(8,128)} %pad.4.ids_ref, bf16[8,2048,1408]{2,1,0:T(8,128)(2,1)} %wg_ref.1, ...), custom_call_target="tpu_custom_call" | custom-call | tf_op jit(solution)/shard_map/gather_up/pallas_call | solution.py:442
  104.4 87.2 %down_sum.1 = bf16[192,2048]{1,0:T(8,128)(2,1)} custom-call(bf16[192,2048]{1,0:T(8,128)(2,1)} %hid_ref.3, bf16[192,2048]{1,0:T(8,128)(2,1)} %get-tuple-element.8.xn_ref, f32[1536,128]{1,0:T(8,128)} %get-tuple-element.9.rg_ref, bf16[8,384,1408]{2,1,0:T(8,128)(2,1)} %get-tuple-element.10.h_ref, bf16[8,1408,2048]{2,1,0:T(8,128)(2,1)} %wd_ref.1, ...), custom_call_target="tpu_custom_call" | custom-call | tf_op jit(solution)/shard_map/down_sum/pallas_call | solution.py:476
  191.6 2.1 %copy.12 = bf16[192,2048]{1,0:T(8,128)(2,1)} copy(bf16[192,2048]{1,0:T(8,128)(2,1)} %down_sum.1) | data formatting | bytes 1572864

commit v2 on v1

v2 whole, which is shorter than its diff:
```python
import functools

import jax
import jax.numpy as jnp
from jax import lax
from jax.experimental import pallas as pl
from jax.experimental.pallas import tpu as pltpu
from jax.sharding import PartitionSpec as P

NORM_EPS = 1e-6
ROUTE_SCALE = 2.5
GROUPS = 8
GROUP_LIMIT = 4
F32 = jnp.float32
BF16 = jnp.bfloat16
VMEM_LIMIT = 67_000_000
TILE = 16


def dot_f32(a, b):
    return jnp.dot(a, b, preferred_element_type=F32)


def place():
    me = lax.axis_index("ep")
    core = lax.rem(me, 2)
    x = lax.rem(me // 2, 2)
    y = me // 4
    return me, core, x, y, me + 1 - 2 * core, me + 2 - 4 * x, me + 4 - 8 * y


def pos_of(dev):
    return lax.rem(dev, 2) * 4 + dev // 2


def rcopy(src, dst, ssem, rsem, dev):
    return pltpu.make_async_remote_copy(
        src_ref=src, dst_ref=dst, send_sem=ssem, recv_sem=rsem, device_id={"ep": dev}, device_id_type=pl.DeviceIdType.MESH
    )


def split3(v):
    hi = v.astype(BF16)
    rest = v - hi.astype(F32)
    mid = rest.astype(BF16)
    return hi, mid, (rest - mid.astype(F32)).astype(BF16)


def iota(shape, axis):
    return lax.broadcasted_iota(jnp.int32, shape, axis)


def gather_up_kernel(
    n_kc, hid_ref, gain_ref, rw_ref, ids_ref, wg_ref, wu_ref, h_ref, rg_ref, xn_ref, tab_ref, back_ref,
    xall, pick, xsrc, acc, wbuf, hbuf, xe, meta_s, meta_r, ids_r, tab_v, tab_s,
    w_sem, h_sem, t_sem, i_send, i_recv, m_send, m_recv, a_send, a_recv,
):
    me, core, x, y, sib, xnb, ynb = place()
    tok, dim = hid_ref.shape
    n_exp, _, inter = wg_ref.shape
    cap = h_ref.shape[1]
    kw = dim // n_kc
    half = tok // 2
    n_steps = n_exp * n_kc
    slots = wbuf.shape[0]
    n_et = cap // TILE
    n_st = pick.shape[1] // TILE

    def w_copies(s):
        e, kc, slot = lax.rem(s, n_exp), s // n_exp, lax.rem(s, slots)
        rows = pl.ds(pl.multiple_of(kc * kw, kw), kw)
        return (
            pltpu.make_async_copy(wg_ref.at[e, rows, :], wbuf.at[slot, :, pl.ds(0, inter)], w_sem.at[slot, 0]),
            pltpu.make_async_copy(wu_ref.at[e, rows, :], wbuf.at[slot, :, pl.ds(inter, inter)], w_sem.at[slot, 1]),
        )

    def w_start(s):
        for c in w_copies(s):
            c.start()

    for s in range(slots - 1):
        w_start(jnp.int32(s))

    barrier = pltpu.get_barrier_semaphore()
    for k in range(1, 8):
        pl.semaphore_signal(barrier, inc=1, device_id={"ep": lax.rem(me + k, 8)}, device_id_type=pl.DeviceIdType.MESH)

    x_f32 = hid_ref[...].astype(F32)
    inv_rms = lax.rsqrt(jnp.mean(x_f32 * x_f32, axis=-1, keepdims=True) + NORM_EPS)
    x_norm = (x_f32 * inv_rms * gain_ref[...]).astype(BF16)
    xn_ref[...] = x_norm
    my_pos = pos_of(me)
    my_rows = pl.ds(pl.multiple_of(my_pos * tok, tok), tok)
    for kc in range(n_kc):
        xall[kc, my_rows, :] = x_norm[:, kc * kw : (kc + 1) * kw]

    pl.semaphore_wait(barrier, 7)

    def block(kc, dev, part=None):
        start = pos_of(dev) * tok + (0 if part is None else part * half)
        n = tok if part is None else half
        return xall.at[kc, pl.ds(pl.multiple_of(start, half), n), :]

    def send(kc, kind, dev_src, to, part=None):
        ref = block(kc, dev_src, part)
        return rcopy(ref, ref, a_send.at[kc, kind], a_recv.at[kc, kind], to)

    diag = me + 6 - 4 * x - 8 * y
    kinds = (
        (me, sib, None), (me, xnb, None), (me, ynb, None), (xnb, ynb, 0), (ynb, xnb, 1),
        (xnb, sib, None), (ynb, sib, None), (diag, sib, 0), (diag, sib, 1),
    )

    def copy(kc, kind):
        src, to, part = kinds[kind]
        return send(kc, kind, src, to, part)

    def start(kc, which):
        for kind in which:
            copy(kc, kind).start()

    def received(kc, which):
        for kind in which:
            copy(kc, kind).wait_recv()

    def serve_a(kc):
        received(kc, (1, 2))
        start(kc, (3, 4, 5, 6))
        if kc + 1 < n_kc:
            start(kc + 1, (1, 2, 0))

    def serve_b(kc):
        received(kc, (3, 4))
        start(kc, (7, 8))

    def meta(k):
        to = lax.rem(me + k, 8)
        return rcopy(meta_s.at[to], meta_r.at[my_pos], m_send.at[k], m_recv.at[k], to)

    def ids_copy(k):
        return rcopy(ids_ref, ids_r.at[my_pos], i_send.at[k], i_recv.at[k], lax.rem(me + k, 8))

    for k in range(1, 8):
        ids_copy(k).start()
    start(0, (1, 2, 0))
    ids_r[pl.ds(my_pos, 1)] = ids_ref[...].reshape(1, 8, 256)

    parts = lax.dot_general(
        jnp.concatenate(split3(rw_ref[...]), axis=0), x_norm, (((1,), (1,)), ((), ())), preferred_element_type=F32
    )
    logits = parts[:64] + (parts[64:128] + parts[128:192])
    scores = jax.nn.sigmoid(logits)
    exp_iota = iota(scores.shape, 0)
    chosen = exp_iota == ids_ref[0:1, :tok]
    for j in range(1, 6):
        chosen = chosen | (exp_iota == ids_ref[j : j + 1, :tok])
    picked = jnp.where(chosen, scores, 0.0)
    gates = ROUTE_SCALE * picked / jnp.sum(picked, axis=0, keepdims=True)
    meta_s[...] = jnp.zeros(meta_s.shape, F32)
    for d in range(8):
        meta_s[d, :, 0:tok] = gates[d * n_exp : (d + 1) * n_exp, :]
    meta_r[pl.ds(my_pos, 1)] = meta_s[pl.ds(me, 1)]
    for k in range(1, 8):
        meta(k).start()
    for k in range(1, 8):
        ids_copy(k).wait_recv()

    my_exp = me * n_exp + iota((n_exp, 256), 0)
    masks = []
    for s in range(8):
        hit = my_exp == ids_r[s, 0:1, :]
        for j in range(1, 6):
            hit = hit | (my_exp == ids_r[s, j : j + 1, :])
        masks.append(hit)
    ones = jnp.concatenate([jnp.where(m, 1.0, 0.0) for m in masks], axis=0).astype(BF16)
    upper = iota((256, 256), 0) <= iota((256, 256), 1)
    cums = dot_f32(ones, jnp.where(upper, 1.0, 0.0).astype(BF16))
    cums = [cums[s * n_exp : (s + 1) * n_exp] for s in range(8)]

    lane = iota((n_exp, 128), 1)
    base = jnp.zeros((n_exp, 128), F32)
    count = jnp.zeros((n_exp, 128), F32)
    before = jnp.zeros((n_exp, 1), F32)
    for s in range(8):
        n = cums[s][:, 255:256]
        base = jnp.where(lane == s, before, base)
        count = jnp.where(lane == s, n, count)
        before = before + n
    base, count = base.astype(jnp.int32), count.astype(jnp.int32)
    first = base // TILE
    tiles = jnp.where(count > 0, (base + count - 1) // TILE - first + 1, 0)
    sub = iota((n_exp, 128), 0)
    ends = tiles
    for d in (1, 2, 4):
        ends = ends + jnp.where(sub >= d, pltpu.roll(ends, d, 0), 0)
    begin = ends - tiles
    shift = ((begin - first) * TILE + base).astype(F32)

    slot_ids = []
    for s in range(8):
        slot_ids.append(jnp.where(masks[s], cums[s] - 1.0 + shift[:, s : s + 1], -1.0))

    def build(s, ids):
        for q in range(0, n_st * TILE, 128):
            want = (iota((128, 256), 0) + q).astype(F32)
            got = want == ids[0:1]
            for e in range(1, n_exp):
                got = got | (want == ids[e : e + 1])
            pick[s, q : q + 128, :] = jnp.where(got, 1.0, 0.0).astype(BF16)[:, :tok]

    for s in range(8):
        build(s, slot_ids[s])

    rows24 = jnp.concatenate([first, tiles, begin], axis=0).astype(F32).astype(BF16)
    src = iota((128, 768), 0)
    col = iota((128, 768), 1)
    spread = jnp.where(jnp.where(col < 256, col % 8, (col - 256) // 64) == src, 1.0, 0.0).astype(BF16)
    table = dot_f32(rows24, spread).astype(jnp.int32)
    t_first, t_tiles, t_begin = table[:n_exp], table[n_exp : 2 * n_exp], table[2 * n_exp :]
    col = iota((n_exp, 256), 1)
    nth = col // 8 - t_first[:, :256]
    valid = (nth >= 0) & (nth < t_tiles[:, :256])
    tab_v[...] = jnp.where(valid, (col % 8) * n_st + t_begin[:, :256] + nth, 8 * n_st)
    out = pltpu.make_async_copy(tab_v, tab_ref, t_sem.at[0])
    out.start()
    nth = iota((n_exp, 512), 1) % 64 - t_begin[:, 256:]
    valid = (nth >= 0) & (nth < t_tiles[:, 256:])
    back = jnp.where(valid, iota((n_exp, 512), 0) * n_et + t_first[:, 256:] + nth, 0)
    back_ref[...] = jnp.sum(back, axis=0, keepdims=True)
    out.wait()
    load = pltpu.make_async_copy(tab_ref, tab_s, t_sem.at[1])
    load.start()

    serve_a(0)

    for k in range(1, 8):
        meta(k).wait_recv()
    for s in range(8):
        packed = jnp.concatenate([slot_ids[s], meta_r[s], jnp.zeros((128 - 2 * n_exp, 256), F32)], axis=0)
        rg_ref[s] = packed.T[:tok]
    xsrc[8 * n_st] = jnp.zeros((TILE, kw), BF16)
    load.wait()

    def select(kc):
        received(kc, (0, 5, 6, 7, 8))

        def one(s, carry):
            rows = xall[kc, pl.ds(pl.multiple_of(s * tok, tok), tok), :]
            res = dot_f32(pick[s], rows).astype(BF16)
            xsrc[pl.ds(s * n_st, n_st)] = res.reshape(n_st, TILE, kw)
            return carry

        lax.fori_loop(0, 8, one, 0)

    def fill(s):
        e, slot = lax.rem(s, n_exp), lax.rem(s, 2)
        for t in range(n_et):
            got = [xsrc[jnp.clip(tab_s[e, t * 8 + k], 0, 8 * n_st)] for k in range(8)]
            while len(got) > 1:
                got = [got[i] + got[i + 1] for i in range(0, len(got), 2)]
            xe[slot, t * TILE : (t + 1) * TILE, :] = got[0]

    serve_b(0)
    select(0)
    fill(jnp.int32(0))

    def step(s, carry):
        e, kc = lax.rem(s, n_exp), s // n_exp
        slot = lax.rem(s, slots)
        for c in range(1, n_kc):
            pl.when(s == n_exp * (c - 1) + 2)(functools.partial(serve_a, c))
            pl.when(s == n_exp * (c - 1) + 5)(functools.partial(serve_b, c))
            pl.when(s == n_exp * c - 1)(functools.partial(select, c))

        @pl.when(s + slots - 1 < n_steps)
        def _():
            w_start(s + slots - 1)

        for c in w_copies(s):
            c.wait()
        fill(s + 1)
        for n in range(0, 2 * inter, 256):
            part = dot_f32(xe[lax.rem(s, 2)], wbuf[slot, :, n : n + 256])
            acc[e, :, n : n + 256] = jnp.where(kc > 0, acc[e, :, n : n + 256], 0.0) + part

        @pl.when(kc == n_kc - 1)
        def _():
            b = lax.rem(e, 2)

            @pl.when(e >= 2)
            def _():
                pltpu.make_async_copy(hbuf.at[b], h_ref.at[e - 2], h_sem.at[b]).wait()

            for n in range(0, inter, 128):
                g = acc[e, :, n : n + 128]
                u = acc[e, :, inter + n : inter + n + 128]
                hbuf[b, :, n : n + 128] = (jax.nn.silu(g) * u).astype(BF16)
            pltpu.make_async_copy(hbuf.at[b], h_ref.at[e], h_sem.at[b]).start()

        return carry

    lax.fori_loop(0, n_steps, step, 0)

    for e in range(n_exp - 2, n_exp):
        pltpu.make_async_copy(hbuf.at[e % 2], h_ref.at[e], h_sem.at[e % 2]).wait()
    for k in range(1, 8):
        ids_copy(k).wait_send()
        meta(k).wait_send()
    for kc in range(n_kc):
        for kind in range(len(kinds)):
            copy(kc, kind).wait_send()


def down_kernel(
    n_chunk, hid_ref, xn_ref, rg_ref, back_ref, h_ref, wd_ref, wsg_ref, wsu_ref, wsd_ref, out_ref,
    hv, weigh, wdb, etile, esrc, part, got0, mid, got1, quart, got2, total, wsb, wdsb, hs,
    hv_sem, wd_sem, ws_sem, wds_sem, d_send, d_recv, p_send, p_recv, q_send, q_recv,
):
    me, core, x, y, sib, xnb, ynb = place()
    n_exp, cap, inter = h_ref.shape
    tok, dim = hid_ref.shape
    n_et = cap // TILE
    n_slot = weigh.shape[-1]
    n_st = n_slot // TILE
    cw = dim // n_chunk
    hw = cw // 2
    unroll = 2
    n_down = n_exp // unroll
    per_src = 4
    per_chunk = n_down + 8 // per_src + 2
    n_steps = n_chunk * per_chunk
    slots = wdb.shape[0]
    sw = wsb.shape[-1] // 2
    n_s = wsg_ref.shape[1] // sw
    dw = wdsb.shape[-1]
    n_d = dim // dw

    def wd_copy(i):
        e, n, slot = lax.rem(i, n_exp), i // n_exp, lax.rem(i, slots)
        return pltpu.make_async_copy(wd_ref.at[e, :, pl.ds(pl.multiple_of(n * cw, cw), cw)], wdb.at[slot], wd_sem.at[slot])

    def h_copy(e):
        return pltpu.make_async_copy(h_ref.at[e], hv.at[e], hv_sem.at[e])

    def ws_copies(i):
        cols = pl.ds(pl.multiple_of(i * sw, sw), sw)
        slot = lax.rem(i, 2)
        return (
            pltpu.make_async_copy(wsg_ref.at[:, cols], wsb.at[slot, :, pl.ds(0, sw)], ws_sem.at[slot, 0]),
            pltpu.make_async_copy(wsu_ref.at[:, cols], wsb.at[slot, :, pl.ds(sw, sw)], ws_sem.at[slot, 1]),
        )

    def wds_copy(i):
        slot = lax.rem(i, 2)
        return pltpu.make_async_copy(wsd_ref.at[:, pl.ds(pl.multiple_of(i * dw, dw), dw)], wdsb.at[slot], wds_sem.at[slot])

    def start(copies):
        for c in copies:
            c.start()

    def wait(copies):
        for c in copies:
            c.wait()

    h_copy(0).start()
    for i in range(slots - unroll):
        wd_copy(jnp.int32(i)).start()
    for e in range(1, n_exp):
        h_copy(e).start()
    start(ws_copies(jnp.int32(0)))

    barrier = pltpu.get_barrier_semaphore()
    for dev in (sib, xnb, ynb):
        pl.semaphore_signal(barrier, inc=1, device_id={"ep": dev}, device_id_type=pl.DeviceIdType.MESH)

    def build(s, carry):
        slot = iota((tok, n_slot), 1).astype(F32)
        val = jnp.zeros((tok, n_slot), F32)
        for e in range(n_exp):
            val = jnp.where(rg_ref[s, :, e : e + 1] == slot, rg_ref[s, :, n_exp + e : n_exp + e + 1], val)
        for k, piece in enumerate(split3(val)):
            weigh[s, k * tok : (k + 1) * tok, :] = piece
        return carry

    lax.fori_loop(0, 8, build, 0)
    pl.semaphore_wait(barrier, 3)

    def d_copy(n):
        b = lax.rem(n, 2)
        return rcopy(part.at[b, :, 1 - core], got0.at[b], d_send.at[b], d_recv.at[b], sib)

    def p_copies(n):
        b = lax.rem(n, 2)
        return (
            rcopy(mid.at[b, 0, :, 1 - x], got1.at[b, 0], p_send.at[b, 0], p_recv.at[b, 0], xnb),
            rcopy(mid.at[b, 1, 1 - y], got1.at[b, 1], p_send.at[b, 1], p_recv.at[b, 1], ynb),
        )

    def q_copies(n):
        b = lax.rem(n, 2)
        return (
            rcopy(quart.at[b, 0, 1 - y], got2.at[b, 0], q_send.at[b, 0], q_recv.at[b, 0], ynb),
            rcopy(quart.at[b, 1, 1 - x], got2.at[b, 1], q_send.at[b, 1], q_recv.at[b, 1], xnb),
        )

    def stage_p(n):
        b = lax.rem(n, 2)
        d_copy(n).wait()
        for hf in range(2):
            for yy in range(2):
                for xx in range(2):
                    rows = pl.ds((yy * 2 + xx) * tok, tok)
                    mid[b, hf, yy, xx] = part[b, hf, core, rows, :] + got0[b, hf, rows, :]
        start(p_copies(n))

    def stage_q(n):
        b = lax.rem(n, 2)
        wait(p_copies(n))
        for k in range(2):
            quart[b, 0, k] = mid[b, 0, k, x] + got1[b, 0, k]
            quart[b, 1, k] = mid[b, 1, y, k] + got1[b, 1, k]
        start(q_copies(n))

    def stage_f(n):
        b = lax.rem(n, 2)
        wait(q_copies(n))
        total[n, 0] = quart[b, 0, y] + got2[b, 0]
        total[n, 1] = quart[b, 1, x] + got2[b, 1]

    def down(n, j):
        i0 = n * n_exp + j * unroll
        for u in range(unroll):
            i = i0 + slots - unroll + u

            @pl.when(i < n_chunk * n_exp)
            def _():
                wd_copy(i).start()

        @pl.when(n == 0)
        def _():
            for u in range(unroll):
                h_copy(j * unroll + u).wait()

        for u in range(unroll):
            wd_copy(i0 + u).wait()
        for u in range(unroll):
            e = j * unroll + u
            res = dot_f32(hv[e], wdb[lax.rem(i0 + u, slots)]).astype(BF16)
            etile[pl.ds(e * n_et, n_et)] = res.reshape(n_et, TILE, cw)

    def combine(n, g):
        b = lax.rem(n, 2)
        for u in range(per_src):
            s = g * per_src + u
            for t in range(n_st):
                esrc[u, t * TILE : (t + 1) * TILE, :] = etile[back_ref[0, s * 64 + t]]
        for u in range(per_src):
            s = g * per_src + u
            res = dot_f32(weigh[s], esrc[u])
            res = res[:tok] + (res[tok : 2 * tok] + res[2 * tok :])
            for hf in range(2):
                part[b, hf, s // 4, pl.ds(pl.multiple_of(lax.rem(s, 4) * tok, tok), tok), :] = res[:, hf * hw : (hf + 1) * hw]

    def shared_up(i):
        @pl.when(i + 1 < n_s)
        def _():
            start(ws_copies(i + 1))

        wait(ws_copies(i))
        both = dot_f32(xn_ref[...], wsb[lax.rem(i, 2)])
        hs[i] = (jax.nn.silu(both[:, :sw]) * both[:, sw:]).astype(BF16)

    def step(s, carry):
        n, j = s // per_chunk, lax.rem(s, per_chunk)
        pl.when(j < n_down)(lambda: down(n, j))

        @pl.when((j >= n_down) & (j < per_chunk - 2))
        def _():
            combine(n, j - n_down)

        pl.when(j == per_chunk - 3)(lambda: d_copy(n).start())
        i = n * 2 + j - (per_chunk - 2)
        pl.when((j >= per_chunk - 2) & (i < n_s))(lambda: shared_up(i))

        @pl.when(j == 0)
        def _():
            pl.when(n >= 3)(lambda: stage_f(n - 3))
            pl.when(n >= 2)(lambda: stage_q(n - 2))
            pl.when(n >= 1)(lambda: stage_p(n - 1))

        return carry

    lax.fori_loop(0, n_steps, step, 0)

    last = jnp.int32(n_chunk - 1)
    wds_copy(jnp.int32(0)).start()
    stage_f(last - 2)
    stage_q(last - 1)
    stage_p(last)
    shared = []
    for i in range(n_d):
        if i + 1 < n_d:
            wds_copy(jnp.int32(i + 1)).start()
        wds_copy(jnp.int32(i)).wait()
        res = jnp.zeros((tok, dw), F32)
        for k in range(n_s):
            res = res + dot_f32(hs[k], wdsb[i % 2, k * sw : (k + 1) * sw, :])
        out_ref[:, i * dw : (i + 1) * dw] = res.astype(BF16)
    stage_f(last - 1)
    stage_q(last)
    stage_f(last)
    for n in range(n_chunk):
        for hf in range(2):
            cols = slice(n * cw + hf * hw, n * cw + (hf + 1) * hw)
            out_ref[:, cols] = (hid_ref[:, cols].astype(F32) + out_ref[:, cols].astype(F32) + total[n, hf]).astype(BF16)


def solution(mesh):
    ep_size = mesh.shape["ep"]
    assert ep_size == 8

    def local_block(hidden_in, norm_gain, router_w, w_gate, w_up, w_down, ws_gate, ws_up, ws_down, expert_ids):
        tok, top_k = expert_ids.shape
        dim = hidden_in.shape[1]
        n_exp, _, inter = w_gate.shape
        s_inter = ws_gate.shape[1]
        cap = GROUPS * ((top_k + GROUP_LIMIT - 1) // GROUP_LIMIT) * tok // n_exp
        n_kc, slots = 4, 3
        kw = dim // n_kc
        pair_cap = cap * n_exp // ep_size
        n_st = (pair_cap + 14 * n_exp) // TILE + n_exp
        n_slot = -(-n_st * TILE // 128) * 128
        n_st = n_slot // TILE
        vmem = pl.BlockSpec(memory_space=pltpu.VMEM)
        smem = pl.BlockSpec(memory_space=pltpu.SMEM)
        hbm = pl.BlockSpec(memory_space=pl.ANY)
        dma = pltpu.SemaphoreType.DMA
        ids_t = jnp.pad(expert_ids.T, ((0, 8 - top_k), (0, 256 - tok)), constant_values=-1)

        h, rg, xn, _, back = pl.pallas_call(
            functools.partial(gather_up_kernel, n_kc),
            out_shape=(
                jax.ShapeDtypeStruct((n_exp, cap, inter), BF16),
                jax.ShapeDtypeStruct((8, tok, 128), F32),
                jax.ShapeDtypeStruct((tok, dim), BF16),
                jax.ShapeDtypeStruct((n_exp, 256), jnp.int32),
                jax.ShapeDtypeStruct((1, 512), jnp.int32),
            ),
            in_specs=[vmem, vmem, vmem, vmem, hbm, hbm],
            out_specs=(hbm, vmem, vmem, hbm, vmem),
            scratch_shapes=[
                pltpu.VMEM((n_kc, 8 * tok, kw), BF16),
                pltpu.VMEM((8, n_slot, tok), BF16),
                pltpu.VMEM((8 * n_st + 1, TILE, kw), BF16),
                pltpu.VMEM((n_exp, cap, 2 * inter), F32),
                pltpu.VMEM((slots, kw, 2 * inter), BF16),
                pltpu.VMEM((2, cap, inter), BF16),
                pltpu.VMEM((2, cap, kw), BF16),
                pltpu.VMEM((8, n_exp, 256), F32),
                pltpu.VMEM((8, n_exp, 256), F32),
                pltpu.VMEM((8, 8, 256), jnp.int32),
                pltpu.VMEM((n_exp, 256), jnp.int32),
                pltpu.SMEM((n_exp, 256), jnp.int32),
                dma((slots, 2)),
                dma((2,)),
                dma((2,)),
                dma((8,)),
                dma((8,)),
                dma((8,)),
                dma((8,)),
                dma((n_kc, 9)),
                dma((n_kc, 9)),
            ],
            compiler_params=pltpu.CompilerParams(collective_id=0, has_side_effects=True, vmem_limit_bytes=VMEM_LIMIT),
            name="gather_up",
        )(hidden_in, norm_gain.reshape(1, dim), router_w, ids_t, w_gate, w_up)

        n_chunk, dslots = 8, 6
        cw = dim // n_chunk
        hw = cw // 2
        sw, dw = 256, 512
        return pl.pallas_call(
            functools.partial(down_kernel, n_chunk),
            out_shape=jax.ShapeDtypeStruct((tok, dim), BF16),
            in_specs=[vmem, vmem, vmem, smem, hbm, hbm, hbm, hbm, hbm],
            out_specs=vmem,
            scratch_shapes=[
                pltpu.VMEM((n_exp, cap, inter), BF16),
                pltpu.VMEM((8, 3 * tok, n_slot), BF16),
                pltpu.VMEM((dslots, inter, cw), BF16),
                pltpu.VMEM((n_exp * cap // TILE, TILE, cw), BF16),
                pltpu.VMEM((4, n_slot, cw), BF16),
                pltpu.VMEM((2, 2, 2, 4 * tok, hw), F32),
                pltpu.VMEM((2, 2, 4 * tok, hw), F32),
                pltpu.VMEM((2, 2, 2, 2, tok, hw), F32),
                pltpu.VMEM((2, 2, 2, tok, hw), F32),
                pltpu.VMEM((2, 2, 2, tok, hw), F32),
                pltpu.VMEM((2, 2, tok, hw), F32),
                pltpu.VMEM((n_chunk, 2, tok, hw), F32),
                pltpu.VMEM((2, dim, 2 * sw), BF16),
                pltpu.VMEM((2, s_inter, dw), BF16),
                pltpu.VMEM((s_inter // sw, tok, sw), BF16),
                dma((n_exp,)),
                dma((dslots,)),
                dma((2, 2)),
                dma((2,)),
                dma((2,)),
                dma((2,)),
                dma((2, 2)),
                dma((2, 2)),
                dma((2, 2)),
                dma((2, 2)),
            ],
            compiler_params=pltpu.CompilerParams(collective_id=1, has_side_effects=True, vmem_limit_bytes=VMEM_LIMIT),
            name="down_sum",
        )(hidden_in, xn, rg, back, h, w_down, ws_gate, ws_up, ws_down)

    row_spec = P(("dp", "ep"), None)
    in_specs = (row_spec, P(), P(), P("ep"), P("ep"), P("ep"), P(), P(), P(), row_spec)
    return jax.shard_map(local_block, mesh=mesh, in_specs=in_specs, out_specs=row_spec, check_vma=False)
```

time: 194 us -> 183 us (0.943)
  Pallas kernels: 190 us -> 179 us
    pallas_call x1, Pallas kernels: 103 us -> 93.3 us  [local_block(): pl.pallas_call(functools.partial(gather_up_kernel, n_kc), out_shape=(jax....]
where the time goes in v2:
time: 183 us; the launch traced here: 182 us
  Pallas kernels  179 us (98%)
  local copies, waits for them, and re-layouts  3.39 us (2%)
    pallas_call x1, Pallas kernels, local_block(): pl.pallas_call(functools.partial(gather_up_kernel, n_kc), out_shape=(jax....  93.3 us
    pallas_call x1, Pallas kernels, local_block(): pl.pallas_call(functools.partial(down_kernel, n_chunk), out_shape=jax.Sha...  85.5 us

profile of v2, /device:TPU:0, one launch (start us, length us, event | category | flops | bytes accessed | tf_op | source)
XLA Modules:
  0.0 182.1 jit_solution(8964046302279615126)
XLA Ops:
  0.0 1.3 pad.4.ids_ref
  1.3 93.3 %gather_up.1 = (bf16[8,384,1408]{2,1,0:T(8,128)(2,1)}, f32[8,192,128]{2,1,0:T(8,128)}, bf16[192,2048]{1,0:T(8,128)(2,1)}, s32[8,256]{1,0:T(8,128)}, s32[1,512]{1,0:T(1,128)}) custom-call(bf16[192,2048]{1,0:T(8,128)(2,1)} %hid_ref.3, f32[1,2048]{1,0:T(1,128)} %bitcast.2, f32[64,2048]{1,0:T(8,128)} %rw_ref.1, s32[8,256]{1,0:T(8,128)} %pad.4.ids_ref, ...), custom_call_target="tpu_custom_call" | custom-call | tf_op jit(solution)/shard_map/gather_up/pallas_call | solution.py:540
  94.6 85.5 %down_sum.1 = bf16[192,2048]{1,0:T(8,128)(2,1)} custom-call(bf16[192,2048]{1,0:T(8,128)(2,1)} %hid_ref.3, bf16[192,2048]{1,0:T(8,128)(2,1)} %get-tuple-element.9.xn_ref, f32[8,192,128]{2,1,0:T(8,128)} %get-tuple-element.10.rg_ref, s32[1,512]{1,0:T(1,128)} %get-tuple-element.11.back_ref, bf16[8,384,1408]{2,1,0:T(8,128)(2,1)} %get-tuple-element.12.h_ref, ...), custom_call_target="tpu_custom_call" | custom-call | tf_op jit(solution)/shard_map/down_sum/pallas_call | solution.py:582
  180.0 2.1 %copy.12 = bf16[192,2048]{1,0:T(8,128)(2,1)} copy(bf16[192,2048]{1,0:T(8,128)(2,1)} %down_sum.1) | data formatting | bytes 1572864

commit v3 on v2

--- a/solution.py
+++ b/solution.py
@@ -53,7 +53,7 @@
 def gather_up_kernel(
     n_kc, hid_ref, gain_ref, rw_ref, ids_ref, wg_ref, wu_ref, h_ref, rg_ref, xn_ref, tab_ref, back_ref,
     xall, pick, xsrc, acc, wbuf, hbuf, xe, meta_s, meta_r, ids_r, tab_v, tab_s,
-    w_sem, h_sem, t_sem, i_send, i_recv, m_send, m_recv, a_send, a_recv,
+    sid, cid, ids_t, w_sem, h_sem, t_sem, x_sem, i_send, i_recv, m_send, m_recv, a_send, a_recv,
 ):
     me, core, x, y, sib, xnb, ynb = place()
     tok, dim = hid_ref.shape
@@ -81,6 +81,9 @@
     for s in range(slots - 1):
         w_start(jnp.int32(s))
 
+    ids_t[...] = jnp.full(ids_t.shape, -1, jnp.int32)
+    ids_t[: ids_ref.shape[0], :tok] = ids_ref[...]
+
     barrier = pltpu.get_barrier_semaphore()
     for k in range(1, 8):
         pl.semaphore_signal(barrier, inc=1, device_id={"ep": lax.rem(me + k, 8)}, device_id_type=pl.DeviceIdType.MESH)
@@ -88,12 +91,16 @@
     x_f32 = hid_ref[...].astype(F32)
     inv_rms = lax.rsqrt(jnp.mean(x_f32 * x_f32, axis=-1, keepdims=True) + NORM_EPS)
     x_norm = (x_f32 * inv_rms * gain_ref[...]).astype(BF16)
-    xn_ref[...] = x_norm
     my_pos = pos_of(me)
     my_rows = pl.ds(pl.multiple_of(my_pos * tok, tok), tok)
     for kc in range(n_kc):
         xall[kc, my_rows, :] = x_norm[:, kc * kw : (kc + 1) * kw]
 
+    def xn_copy(kc):
+        return pltpu.make_async_copy(xall.at[kc, my_rows, :], xn_ref.at[:, pl.ds(kc * kw, kw)], x_sem.at[kc])
+
+    for kc in range(n_kc):
+        xn_copy(kc).start()
     pl.semaphore_wait(barrier, 7)
 
     def block(kc, dev, part=None):
@@ -126,8 +133,7 @@
     def serve_a(kc):
         received(kc, (1, 2))
         start(kc, (3, 4, 5, 6))
-        if kc + 1 < n_kc:
-            start(kc + 1, (1, 2, 0))
+        pl.when(kc + 1 < n_kc)(lambda: start(kc + 1, (1, 2, 0)))
 
     def serve_b(kc):
         received(kc, (3, 4))
@@ -138,12 +144,12 @@
         return rcopy(meta_s.at[to], meta_r.at[my_pos], m_send.at[k], m_recv.at[k], to)
 
     def ids_copy(k):
-        return rcopy(ids_ref, ids_r.at[my_pos], i_send.at[k], i_recv.at[k], lax.rem(me + k, 8))
+        return rcopy(ids_t, ids_r.at[my_pos], i_send.at[k], i_recv.at[k], lax.rem(me + k, 8))
 
     for k in range(1, 8):
         ids_copy(k).start()
     start(0, (1, 2, 0))
-    ids_r[pl.ds(my_pos, 1)] = ids_ref[...].reshape(1, 8, 256)
+    ids_r[pl.ds(my_pos, 1)] = ids_t[...].reshape(1, 8, 256)
 
     parts = lax.dot_general(
         jnp.concatenate(split3(rw_ref[...]), axis=0), x_norm, (((1,), (1,)), ((), ())), preferred_element_type=F32
@@ -151,9 +157,9 @@
     logits = parts[:64] + (parts[64:128] + parts[128:192])
     scores = jax.nn.sigmoid(logits)
     exp_iota = iota(scores.shape, 0)
-    chosen = exp_iota == ids_ref[0:1, :tok]
+    chosen = exp_iota == ids_t[0:1, :tok]
     for j in range(1, 6):
-        chosen = chosen | (exp_iota == ids_ref[j : j + 1, :tok])
+        chosen = chosen | (exp_iota == ids_t[j : j + 1, :tok])
     picked = jnp.where(chosen, scores, 0.0)
     gates = ROUTE_SCALE * picked / jnp.sum(picked, axis=0, keepdims=True)
     meta_s[...] = jnp.zeros(meta_s.shape, F32)
@@ -196,20 +202,26 @@
     begin = ends - tiles
     shift = ((begin - first) * TILE + base).astype(F32)
 
-    slot_ids = []
     for s in range(8):
-        slot_ids.append(jnp.where(masks[s], cums[s] - 1.0 + shift[:, s : s + 1], -1.0))
-
-    def build(s, ids):
+        slot_id = jnp.where(masks[s], cums[s] - 1.0 + shift[:, s : s + 1], -1.0)
+        sid[s] = slot_id
+        by_col = jnp.full((8, 256), -1.0, F32)
+        for e in range(n_exp):
+            by_col = jnp.where(ids_r[s] == me * n_exp + e, slot_id[e : e + 1], by_col)
+        cid[s] = by_col
+
+    def build(s, carry):
         for q in range(0, n_st * TILE, 128):
             want = (iota((128, 256), 0) + q).astype(F32)
-            got = want == ids[0:1]
-            for e in range(1, n_exp):
-                got = got | (want == ids[e : e + 1])
+            got = want == cid[s, 0:1, :]
+            for j in range(1, 6):
+                got = got | (want == cid[s, j : j + 1, :])
             pick[s, q : q + 128, :] = jnp.where(got, 1.0, 0.0).astype(BF16)[:, :tok]
-
-    for s in range(8):
-        build(s, slot_ids[s])
+        return carry
+
+    lax.fori_loop(0, 4, build, 0)
+    serve_a(0)
+    lax.fori_loop(4, 8, build, 0)
 
     rows24 = jnp.concatenate([first, tiles, begin], axis=0).astype(F32).astype(BF16)
     src = iota((128, 768), 0)
@@ -220,7 +232,7 @@
     col = iota((n_exp, 256), 1)
     nth = col // 8 - t_first[:, :256]
     valid = (nth >= 0) & (nth < t_tiles[:, :256])
-    tab_v[...] = jnp.where(valid, (col % 8) * n_st + t_begin[:, :256] + nth, 8 * n_st)
+    tab_v[...] = jnp.where(valid, t_begin[:, :256] + nth, n_st - 1)
     out = pltpu.make_async_copy(tab_v, tab_ref, t_sem.at[0])
     out.start()
     nth = iota((n_exp, 512), 1) % 64 - t_begin[:, 256:]
@@ -231,31 +243,20 @@
     load = pltpu.make_async_copy(tab_ref, tab_s, t_sem.at[1])
     load.start()
 
-    serve_a(0)
-
-    for k in range(1, 8):
-        meta(k).wait_recv()
-    for s in range(8):
-        packed = jnp.concatenate([slot_ids[s], meta_r[s], jnp.zeros((128 - 2 * n_exp, 256), F32)], axis=0)
-        rg_ref[s] = packed.T[:tok]
-    xsrc[8 * n_st] = jnp.zeros((TILE, kw), BF16)
     load.wait()
 
     def select(kc):
         received(kc, (0, 5, 6, 7, 8))
 
-        def one(s, carry):
-            rows = xall[kc, pl.ds(pl.multiple_of(s * tok, tok), tok), :]
-            res = dot_f32(pick[s], rows).astype(BF16)
-            xsrc[pl.ds(s * n_st, n_st)] = res.reshape(n_st, TILE, kw)
-            return carry
-
-        lax.fori_loop(0, 8, one, 0)
+        for s in range(8):
+            for n in range(0, kw, 256):
+                res = dot_f32(pick[s], xall[kc, s * tok : (s + 1) * tok, n : n + 256]).astype(BF16)
+                xsrc[s * n_st : (s + 1) * n_st, :, n : n + 256] = res.reshape(n_st, TILE, 256)
 
     def fill(s):
         e, slot = lax.rem(s, n_exp), lax.rem(s, 2)
         for t in range(n_et):
-            got = [xsrc[jnp.clip(tab_s[e, t * 8 + k], 0, 8 * n_st)] for k in range(8)]
+            got = [xsrc[k * n_st + (tab_s[e, t * 8 + k] & 63)] for k in range(8)]
             while len(got) > 1:
                 got = [got[i] + got[i + 1] for i in range(0, len(got), 2)]
             xe[slot, t * TILE : (t + 1) * TILE, :] = got[0]
@@ -267,10 +268,10 @@
     def step(s, carry):
         e, kc = lax.rem(s, n_exp), s // n_exp
         slot = lax.rem(s, slots)
-        for c in range(1, n_kc):
-            pl.when(s == n_exp * (c - 1) + 2)(functools.partial(serve_a, c))
-            pl.when(s == n_exp * (c - 1) + 5)(functools.partial(serve_b, c))
-            pl.when(s == n_exp * c - 1)(functools.partial(select, c))
+        more = kc + 1 < n_kc
+        pl.when(more & (e == 2))(lambda: serve_a(kc + 1))
+        pl.when(more & (e == 5))(lambda: serve_b(kc + 1))
+        pl.when(more & (e == n_exp - 1))(lambda: select(kc + 1))
 
         @pl.when(s + slots - 1 < n_steps)
         def _():
@@ -303,6 +304,13 @@
 
     for e in range(n_exp - 2, n_exp):
         pltpu.make_async_copy(hbuf.at[e % 2], h_ref.at[e], h_sem.at[e % 2]).wait()
+    for k in range(1, 8):
+        meta(k).wait_recv()
+    for s in range(8):
+        rg_ref[s, :n_exp] = sid[s]
+        rg_ref[s, n_exp:] = meta_r[s]
+    for kc in range(n_kc):
+        xn_copy(kc).wait()
     for k in range(1, 8):
         ids_copy(k).wait_send()
         meta(k).wait_send()
@@ -344,7 +352,7 @@
 
     def ws_copies(i):
         cols = pl.ds(pl.multiple_of(i * sw, sw), sw)
-        slot = lax.rem(i, 2)
+        slot = lax.rem(i, wsb.shape[0])
         return (
             pltpu.make_async_copy(wsg_ref.at[:, cols], wsb.at[slot, :, pl.ds(0, sw)], ws_sem.at[slot, 0]),
             pltpu.make_async_copy(wsu_ref.at[:, cols], wsb.at[slot, :, pl.ds(sw, sw)], ws_sem.at[slot, 1]),
@@ -367,7 +375,8 @@
         wd_copy(jnp.int32(i)).start()
     for e in range(1, n_exp):
         h_copy(e).start()
-    start(ws_copies(jnp.int32(0)))
+    for i in range(wsb.shape[0] - 1):
+        start(ws_copies(jnp.int32(i)))
 
     barrier = pltpu.get_barrier_semaphore()
     for dev in (sib, xnb, ynb):
@@ -376,8 +385,9 @@
     def build(s, carry):
         slot = iota((tok, n_slot), 1).astype(F32)
         val = jnp.zeros((tok, n_slot), F32)
+        cols = jnp.concatenate([rg_ref[s], jnp.zeros((128 - 2 * n_exp, 256), F32)], axis=0).T[:tok]
         for e in range(n_exp):
-            val = jnp.where(rg_ref[s, :, e : e + 1] == slot, rg_ref[s, :, n_exp + e : n_exp + e + 1], val)
+            val = jnp.where(cols[:, e : e + 1] == slot, cols[:, n_exp + e : n_exp + e + 1], val)
         for k, piece in enumerate(split3(val)):
             weigh[s, k * tok : (k + 1) * tok, :] = piece
         return carry
@@ -390,31 +400,31 @@
         return rcopy(part.at[b, :, 1 - core], got0.at[b], d_send.at[b], d_recv.at[b], sib)
 
     def p_copies(n):
-        b = lax.rem(n, 2)
+        b = lax.rem(n, 4)
         return (
             rcopy(mid.at[b, 0, :, 1 - x], got1.at[b, 0], p_send.at[b, 0], p_recv.at[b, 0], xnb),
             rcopy(mid.at[b, 1, 1 - y], got1.at[b, 1], p_send.at[b, 1], p_recv.at[b, 1], ynb),
         )
 
     def q_copies(n):
-        b = lax.rem(n, 2)
+        b = lax.rem(n, 4)
         return (
             rcopy(quart.at[b, 0, 1 - y], got2.at[b, 0], q_send.at[b, 0], q_recv.at[b, 0], ynb),
             rcopy(quart.at[b, 1, 1 - x], got2.at[b, 1], q_send.at[b, 1], q_recv.at[b, 1], xnb),
         )
 
     def stage_p(n):
-        b = lax.rem(n, 2)
+        b, b4 = lax.rem(n, 2), lax.rem(n, 4)
         d_copy(n).wait()
         for hf in range(2):
             for yy in range(2):
                 for xx in range(2):
                     rows = pl.ds((yy * 2 + xx) * tok, tok)
-                    mid[b, hf, yy, xx] = part[b, hf, core, rows, :] + got0[b, hf, rows, :]
+                    mid[b4, hf, yy, xx] = part[b, hf, core, rows, :] + got0[b, hf, rows, :]
         start(p_copies(n))
 
     def stage_q(n):
-        b = lax.rem(n, 2)
+        b = lax.rem(n, 4)
         wait(p_copies(n))
         for k in range(2):
             quart[b, 0, k] = mid[b, 0, k, x] + got1[b, 0, k]
@@ -422,7 +432,7 @@
         start(q_copies(n))
 
     def stage_f(n):
-        b = lax.rem(n, 2)
+        b = lax.rem(n, 4)
         wait(q_copies(n))
         total[n, 0] = quart[b, 0, y] + got2[b, 0]
         total[n, 1] = quart[b, 1, x] + got2[b, 1]
@@ -462,12 +472,14 @@
                 part[b, hf, s // 4, pl.ds(pl.multiple_of(lax.rem(s, 4) * tok, tok), tok), :] = res[:, hf * hw : (hf + 1) * hw]
 
     def shared_up(i):
-        @pl.when(i + 1 < n_s)
+        ahead = i + wsb.shape[0] - 1
+
+        @pl.when(ahead < n_s)
         def _():
-            start(ws_copies(i + 1))
+            start(ws_copies(ahead))
 
         wait(ws_copies(i))
-        both = dot_f32(xn_ref[...], wsb[lax.rem(i, 2)])
+        both = dot_f32(xn_ref[...], wsb[lax.rem(i, wsb.shape[0])])
         hs[i] = (jax.nn.silu(both[:, :sw]) * both[:, sw:]).astype(BF16)
 
     def step(s, carry):
@@ -484,9 +496,10 @@
 
         @pl.when(j == 0)
         def _():
-            pl.when(n >= 3)(lambda: stage_f(n - 3))
-            pl.when(n >= 2)(lambda: stage_q(n - 2))
             pl.when(n >= 1)(lambda: stage_p(n - 1))
+            pl.when(n >= 4)(lambda: stage_f(n - 4))
+
+        pl.when((j == n_down - 1) & (n >= 2))(lambda: stage_q(n - 2))
 
         return carry
 
@@ -494,10 +507,10 @@
 
     last = jnp.int32(n_chunk - 1)
     wds_copy(jnp.int32(0)).start()
+    stage_p(last)
+    stage_q(last - 1)
+    stage_f(last - 3)
     stage_f(last - 2)
-    stage_q(last - 1)
-    stage_p(last)
-    shared = []
     for i in range(n_d):
         if i + 1 < n_d:
             wds_copy(jnp.int32(i + 1)).start()
@@ -529,29 +542,28 @@
         kw = dim // n_kc
         pair_cap = cap * n_exp // ep_size
         n_st = (pair_cap + 14 * n_exp) // TILE + n_exp
-        n_slot = -(-n_st * TILE // 128) * 128
+        n_slot = -(-(n_st + 1) * TILE // 128) * 128
         n_st = n_slot // TILE
+        assert n_st <= 64
         vmem = pl.BlockSpec(memory_space=pltpu.VMEM)
         smem = pl.BlockSpec(memory_space=pltpu.SMEM)
         hbm = pl.BlockSpec(memory_space=pl.ANY)
         dma = pltpu.SemaphoreType.DMA
-        ids_t = jnp.pad(expert_ids.T, ((0, 8 - top_k), (0, 256 - tok)), constant_values=-1)
-
         h, rg, xn, _, back = pl.pallas_call(
             functools.partial(gather_up_kernel, n_kc),
             out_shape=(
                 jax.ShapeDtypeStruct((n_exp, cap, inter), BF16),
-                jax.ShapeDtypeStruct((8, tok, 128), F32),
+                jax.ShapeDtypeStruct((8, 2 * n_exp, 256), F32),
                 jax.ShapeDtypeStruct((tok, dim), BF16),
                 jax.ShapeDtypeStruct((n_exp, 256), jnp.int32),
                 jax.ShapeDtypeStruct((1, 512), jnp.int32),
             ),
             in_specs=[vmem, vmem, vmem, vmem, hbm, hbm],
-            out_specs=(hbm, vmem, vmem, hbm, vmem),
+            out_specs=(hbm, vmem, hbm, hbm, vmem),
             scratch_shapes=[
                 pltpu.VMEM((n_kc, 8 * tok, kw), BF16),
                 pltpu.VMEM((8, n_slot, tok), BF16),
-                pltpu.VMEM((8 * n_st + 1, TILE, kw), BF16),
+                pltpu.VMEM((7 * n_st + 64, TILE, kw), BF16),
                 pltpu.VMEM((n_exp, cap, 2 * inter), F32),
                 pltpu.VMEM((slots, kw, 2 * inter), BF16),
                 pltpu.VMEM((2, cap, inter), BF16),
@@ -561,9 +573,13 @@
                 pltpu.VMEM((8, 8, 256), jnp.int32),
                 pltpu.VMEM((n_exp, 256), jnp.int32),
                 pltpu.SMEM((n_exp, 256), jnp.int32),
+                pltpu.VMEM((8, n_exp, 256), F32),
+                pltpu.VMEM((8, n_exp, 256), F32),
+                pltpu.VMEM((8, 256), jnp.int32),
                 dma((slots, 2)),
                 dma((2,)),
                 dma((2,)),
+                dma((n_kc,)),
                 dma((8,)),
                 dma((8,)),
                 dma((8,)),
@@ -573,9 +589,9 @@
             ],
             compiler_params=pltpu.CompilerParams(collective_id=0, has_side_effects=True, vmem_limit_bytes=VMEM_LIMIT),
             name="gather_up",
-        )(hidden_in, norm_gain.reshape(1, dim), router_w, ids_t, w_gate, w_up)
-
-        n_chunk, dslots = 8, 6
+        )(hidden_in, norm_gain.reshape(1, dim), router_w, expert_ids.T, w_gate, w_up)
+
+        n_chunk, dslots = 8, 14
         cw = dim // n_chunk
         hw = cw // 2
         sw, dw = 256, 512
@@ -592,24 +608,24 @@
                 pltpu.VMEM((4, n_slot, cw), BF16),
                 pltpu.VMEM((2, 2, 2, 4 * tok, hw), F32),
                 pltpu.VMEM((2, 2, 4 * tok, hw), F32),
-                pltpu.VMEM((2, 2, 2, 2, tok, hw), F32),
-                pltpu.VMEM((2, 2, 2, tok, hw), F32),
-                pltpu.VMEM((2, 2, 2, tok, hw), F32),
-                pltpu.VMEM((2, 2, tok, hw), F32),
+                pltpu.VMEM((4, 2, 2, 2, tok, hw), F32),
+                pltpu.VMEM((4, 2, 2, tok, hw), F32),
+                pltpu.VMEM((4, 2, 2, tok, hw), F32),
+                pltpu.VMEM((4, 2, tok, hw), F32),
                 pltpu.VMEM((n_chunk, 2, tok, hw), F32),
-                pltpu.VMEM((2, dim, 2 * sw), BF16),
+                pltpu.VMEM((3, dim, 2 * sw), BF16),
                 pltpu.VMEM((2, s_inter, dw), BF16),
                 pltpu.VMEM((s_inter // sw, tok, sw), BF16),
                 dma((n_exp,)),
                 dma((dslots,)),
-                dma((2, 2)),
+                dma((3, 2)),
                 dma((2,)),
                 dma((2,)),
                 dma((2,)),
-                dma((2, 2)),
-                dma((2, 2)),
-                dma((2, 2)),
-                dma((2, 2)),
+                dma((4, 2)),
+                dma((4, 2)),
+                dma((4, 2)),
+                dma((4, 2)),
             ],
             compiler_params=pltpu.CompilerParams(collective_id=1, has_side_effects=True, vmem_limit_bytes=VMEM_LIMIT),
             name="down_sum",

time: 183 us -> 163 us (0.89)
  Pallas kernels: 179 us -> 160 us
    pallas_call x1, Pallas kernels: 93.3 us -> 80 us  [local_block(): pl.pallas_call(functools.partial(gather_up_kernel, n_kc), out_shape=(jax....]
    pallas_call x1, Pallas kernels: 85.5 us -> 80.5 us  [local_block(): pl.pallas_call(functools.partial(down_kernel, n_chunk), out_shape=jax.Sha...]
where the time goes in v3:
time: 163 us
  Pallas kernels  160 us (98%)
  local copies, waits for them, and re-layouts  2.09 us (1%)
    pallas_call x1, Pallas kernels, local_block(): pl.pallas_call(functools.partial(down_kernel, n_chunk), out_shape=jax.Sha...  80.5 us
    pallas_call x1, Pallas kernels, local_block(): pl.pallas_call(functools.partial(gather_up_kernel, n_kc), out_shape=(jax....  80 us

profile of v3, /device:TPU:0, one launch (start us, length us, event | category | flops | bytes accessed | tf_op | source)
XLA Modules:
  0.0 162.6 jit_solution(16312452812256415925)
XLA Ops:
  0.0 80.0 %gather_up.1 = (bf16[8,384,1408]{2,1,0:T(8,128)(2,1)}, f32[8,16,256]{2,1,0:T(8,128)}, bf16[192,2048]{1,0:T(8,128)(2,1)}, s32[8,256]{1,0:T(8,128)}, s32[1,512]{1,0:T(1,128)}) custom-call(bf16[192,2048]{1,0:T(8,128)(2,1)} %hid_ref.3, f32[1,2048]{1,0:T(1,128)} %bitcast.2, f32[64,2048]{1,0:T(8,128)} %rw_ref.1, s32[6,192]{1,0:T(8,128)} %bitcast.3, ...), custom_call_target="tpu_custom_call" | custom-call | tf_op jit(solution)/shard_map/gather_up/pallas_call | solution.py:552
  80.0 80.5 %down_sum.1 = bf16[192,2048]{1,0:T(8,128)(2,1)} custom-call(bf16[192,2048]{1,0:T(8,128)(2,1)} %hid_ref.3, bf16[192,2048]{1,0:T(8,128)(2,1)} %get-tuple-element.9.xn_ref, f32[8,16,256]{2,1,0:T(8,128)} %get-tuple-element.10.rg_ref, s32[1,512]{1,0:T(1,128)} %get-tuple-element.11.back_ref, bf16[8,384,1408]{2,1,0:T(8,128)(2,1)} %get-tuple-element.12.h_ref, ...), custom_call_target="tpu_custom_call" | custom-call | tf_op jit(solution)/shard_map/down_sum/pallas_call | solution.py:598
  160.5 2.1 %copy.12 = bf16[192,2048]{1,0:T(8,128)(2,1)} copy(bf16[192,2048]{1,0:T(8,128)(2,1)} %down_sum.1) | data formatting | bytes 1572864

commit v4 on v3

--- a/solution.py
+++ b/solution.py
@@ -210,19 +210,6 @@
             by_col = jnp.where(ids_r[s] == me * n_exp + e, slot_id[e : e + 1], by_col)
         cid[s] = by_col
 
-    def build(s, carry):
-        for q in range(0, n_st * TILE, 128):
-            want = (iota((128, 256), 0) + q).astype(F32)
-            got = want == cid[s, 0:1, :]
-            for j in range(1, 6):
-                got = got | (want == cid[s, j : j + 1, :])
-            pick[s, q : q + 128, :] = jnp.where(got, 1.0, 0.0).astype(BF16)[:, :tok]
-        return carry
-
-    lax.fori_loop(0, 4, build, 0)
-    serve_a(0)
-    lax.fori_loop(4, 8, build, 0)
-
     rows24 = jnp.concatenate([first, tiles, begin], axis=0).astype(F32).astype(BF16)
     src = iota((128, 768), 0)
     col = iota((128, 768), 1)
@@ -239,10 +226,22 @@
     valid = (nth >= 0) & (nth < t_tiles[:, 256:])
     back = jnp.where(valid, iota((n_exp, 512), 0) * n_et + t_first[:, 256:] + nth, 0)
     back_ref[...] = jnp.sum(back, axis=0, keepdims=True)
+
+    def build(s, carry):
+        for q in range(0, n_st * TILE, 128):
+            want = (iota((128, 256), 0) + q).astype(F32)
+            got = want == cid[s, 0:1, :]
+            for j in range(1, 6):
+                got = got | (want == cid[s, j : j + 1, :])
+            pick[s, q : q + 128, :] = jnp.where(got, 1.0, 0.0).astype(BF16)[:, :tok]
+        return carry
+
+    lax.fori_loop(0, 4, build, 0)
     out.wait()
     load = pltpu.make_async_copy(tab_ref, tab_s, t_sem.at[1])
     load.start()
-
+    serve_a(0)
+    lax.fori_loop(4, 8, build, 0)
     load.wait()
 
     def select(kc):
@@ -279,10 +278,14 @@
 
         for c in w_copies(s):
             c.wait()
-        fill(s + 1)
-        for n in range(0, 2 * inter, 256):
-            part = dot_f32(xe[lax.rem(s, 2)], wbuf[slot, :, n : n + 256])
-            acc[e, :, n : n + 256] = jnp.where(kc > 0, acc[e, :, n : n + 256], 0.0) + part
+        rows = xe.at[lax.rem(s, 2)]
+
+        @pl.when(kc < n_kc - 1)
+        def _():
+            fill(s + 1)
+            for n in range(0, 2 * inter, 256):
+                part = dot_f32(rows[...], wbuf[slot, :, n : n + 256])
+                acc[e, :, n : n + 256] = jnp.where(kc > 0, acc[e, :, n : n + 256], 0.0) + part
 
         @pl.when(kc == n_kc - 1)
         def _():
@@ -292,10 +295,12 @@
             def _():
                 pltpu.make_async_copy(hbuf.at[b], h_ref.at[e - 2], h_sem.at[b]).wait()
 
-            for n in range(0, inter, 128):
-                g = acc[e, :, n : n + 128]
-                u = acc[e, :, inter + n : inter + n + 128]
-                hbuf[b, :, n : n + 128] = (jax.nn.silu(g) * u).astype(BF16)
+            fill(s + 1)
+            for n in range(0, inter, 256):
+                w = min(256, inter - n)
+                g = acc[e, :, n : n + w] + dot_f32(rows[...], wbuf[slot, :, n : n + w])
+                u = acc[e, :, inter + n : inter + n + w] + dot_f32(rows[...], wbuf[slot, :, inter + n : inter + n + w])
+                hbuf[b, :, n : n + w] = (jax.nn.silu(g) * u).astype(BF16)
             pltpu.make_async_copy(hbuf.at[b], h_ref.at[e], h_sem.at[b]).start()
 
         return carry
@@ -335,7 +340,7 @@
     unroll = 2
     n_down = n_exp // unroll
     per_src = 4
-    per_chunk = n_down + 8 // per_src + 2
+    per_chunk = n_down + 8 // per_src
     n_steps = n_chunk * per_chunk
     slots = wdb.shape[0]
     sw = wsb.shape[-1] // 2
@@ -377,6 +382,8 @@
         h_copy(e).start()
     for i in range(wsb.shape[0] - 1):
         start(ws_copies(jnp.int32(i)))
+    for i in range(2):
+        wds_copy(jnp.int32(i)).start()
 
     barrier = pltpu.get_barrier_semaphore()
     for dev in (sib, xnb, ynb):
@@ -402,8 +409,8 @@
     def p_copies(n):
         b = lax.rem(n, 4)
         return (
-            rcopy(mid.at[b, 0, :, 1 - x], got1.at[b, 0], p_send.at[b, 0], p_recv.at[b, 0], xnb),
-            rcopy(mid.at[b, 1, 1 - y], got1.at[b, 1], p_send.at[b, 1], p_recv.at[b, 1], ynb),
+            rcopy(mid.at[lax.rem(n, 2), 0, :, 1 - x], got1.at[b, 0], p_send.at[b, 0], p_recv.at[b, 0], xnb),
+            rcopy(mid.at[lax.rem(n, 2), 1, 1 - y], got1.at[b, 1], p_send.at[b, 1], p_recv.at[b, 1], ynb),
         )
 
     def q_copies(n):
@@ -414,21 +421,21 @@
         )
 
     def stage_p(n):
-        b, b4 = lax.rem(n, 2), lax.rem(n, 4)
+        b = lax.rem(n, 2)
         d_copy(n).wait()
         for hf in range(2):
             for yy in range(2):
                 for xx in range(2):
                     rows = pl.ds((yy * 2 + xx) * tok, tok)
-                    mid[b4, hf, yy, xx] = part[b, hf, core, rows, :] + got0[b, hf, rows, :]
+                    mid[b, hf, yy, xx] = part[b, hf, core, rows, :] + got0[b, hf, rows, :]
         start(p_copies(n))
 
     def stage_q(n):
         b = lax.rem(n, 4)
         wait(p_copies(n))
         for k in range(2):
-            quart[b, 0, k] = mid[b, 0, k, x] + got1[b, 0, k]
-            quart[b, 1, k] = mid[b, 1, y, k] + got1[b, 1, k]
+            quart[b, 0, k] = mid[lax.rem(n, 2), 0, k, x] + got1[b, 0, k]
+            quart[b, 1, k] = mid[lax.rem(n, 2), 1, y, k] + got1[b, 1, k]
         start(q_copies(n))
 
     def stage_f(n):
@@ -485,42 +492,46 @@
     def step(s, carry):
         n, j = s // per_chunk, lax.rem(s, per_chunk)
         pl.when(j < n_down)(lambda: down(n, j))
-
-        @pl.when((j >= n_down) & (j < per_chunk - 2))
-        def _():
-            combine(n, j - n_down)
-
-        pl.when(j == per_chunk - 3)(lambda: d_copy(n).start())
-        i = n * 2 + j - (per_chunk - 2)
-        pl.when((j >= per_chunk - 2) & (i < n_s))(lambda: shared_up(i))
-
-        @pl.when(j == 0)
+        pl.when(j >= n_down)(lambda: combine(n, j - n_down))
+        pl.when(j == per_chunk - 1)(lambda: d_copy(n).start())
+
+        @pl.when(j == 1)
         def _():
             pl.when(n >= 1)(lambda: stage_p(n - 1))
             pl.when(n >= 4)(lambda: stage_f(n - 4))
 
-        pl.when((j == n_down - 1) & (n >= 2))(lambda: stage_q(n - 2))
+        pl.when((j == n_down) & (n >= 2))(lambda: stage_q(n - 2))
 
         return carry
 
     lax.fori_loop(0, n_steps, step, 0)
 
     last = jnp.int32(n_chunk - 1)
-    wds_copy(jnp.int32(0)).start()
-    stage_p(last)
-    stage_q(last - 1)
-    stage_f(last - 3)
-    stage_f(last - 2)
+
+    def up_step(i, carry):
+        shared_up(i)
+        pl.when(i == 1)(lambda: stage_p(last))
+        pl.when(i == 4)(lambda: stage_q(last - 1))
+
+        @pl.when(i == 8)
+        def _():
+            stage_f(last - 3)
+            stage_f(last - 2)
+
+        return carry
+
+    lax.fori_loop(0, n_s, up_step, 0)
     for i in range(n_d):
-        if i + 1 < n_d:
-            wds_copy(jnp.int32(i + 1)).start()
         wds_copy(jnp.int32(i)).wait()
         res = jnp.zeros((tok, dw), F32)
         for k in range(n_s):
             res = res + dot_f32(hs[k], wdsb[i % 2, k * sw : (k + 1) * sw, :])
         out_ref[:, i * dw : (i + 1) * dw] = res.astype(BF16)
+        if i + 2 < n_d:
+            wds_copy(jnp.int32(i + 2)).start()
+        if i == 1:
+            stage_q(last)
     stage_f(last - 1)
-    stage_q(last)
     stage_f(last)
     for n in range(n_chunk):
         for hf in range(2):
@@ -591,7 +602,7 @@
             name="gather_up",
         )(hidden_in, norm_gain.reshape(1, dim), router_w, expert_ids.T, w_gate, w_up)
 
-        n_chunk, dslots = 8, 14
+        n_chunk, dslots = 8, 8
         cw = dim // n_chunk
         hw = cw // 2
         sw, dw = 256, 512
@@ -608,17 +619,17 @@
                 pltpu.VMEM((4, n_slot, cw), BF16),
                 pltpu.VMEM((2, 2, 2, 4 * tok, hw), F32),
                 pltpu.VMEM((2, 2, 4 * tok, hw), F32),
-                pltpu.VMEM((4, 2, 2, 2, tok, hw), F32),
+                pltpu.VMEM((2, 2, 2, 2, tok, hw), F32),
                 pltpu.VMEM((4, 2, 2, tok, hw), F32),
                 pltpu.VMEM((4, 2, 2, tok, hw), F32),
                 pltpu.VMEM((4, 2, tok, hw), F32),
                 pltpu.VMEM((n_chunk, 2, tok, hw), F32),
-                pltpu.VMEM((3, dim, 2 * sw), BF16),
+                pltpu.VMEM((5, dim, 2 * sw), BF16),
                 pltpu.VMEM((2, s_inter, dw), BF16),
                 pltpu.VMEM((s_inter // sw, tok, sw), BF16),
                 dma((n_exp,)),
                 dma((dslots,)),
-                dma((3, 2)),
+                dma((5, 2)),
                 dma((2,)),
                 dma((2,)),
                 dma((2,)),

time: 163 us -> 155 us (0.951)
  Pallas kernels: 160 us -> 152 us
    pallas_call x1, Pallas kernels: 80.5 us -> 73.5 us  [local_block(): pl.pallas_call(functools.partial(down_kernel, n_chunk), out_shape=jax.Sha...]
where the time goes in v4:
time: 155 us; the launch traced here: 154 us
  Pallas kernels  152 us (98%)
  local copies, waits for them, and re-layouts  2.09 us (1%)
    pallas_call x1, Pallas kernels, local_block(): pl.pallas_call(functools.partial(gather_up_kernel, n_kc), out_shape=(jax....  78.7 us
    pallas_call x1, Pallas kernels, local_block(): pl.pallas_call(functools.partial(down_kernel, n_chunk), out_shape=jax.Sha...  73.5 us

profile of v4, /device:TPU:0, one launch (start us, length us, event | category | flops | bytes accessed | tf_op | source)
XLA Modules:
  0.0 154.4 jit_solution(9663687414466522682)
XLA Ops:
  0.0 78.7 %gather_up.1 = (bf16[8,384,1408]{2,1,0:T(8,128)(2,1)}, f32[8,16,256]{2,1,0:T(8,128)}, bf16[192,2048]{1,0:T(8,128)(2,1)}, s32[8,256]{1,0:T(8,128)}, s32[1,512]{1,0:T(1,128)}) custom-call(bf16[192,2048]{1,0:T(8,128)(2,1)} %hid_ref.3, f32[1,2048]{1,0:T(1,128)} %bitcast.2, f32[64,2048]{1,0:T(8,128)} %rw_ref.1, s32[6,192]{1,0:T(8,128)} %bitcast.3, ...), custom_call_target="tpu_custom_call" | custom-call | tf_op jit(solution)/shard_map/gather_up/pallas_call | solution.py:563
  78.7 73.5 %down_sum.1 = bf16[192,2048]{1,0:T(8,128)(2,1)} custom-call(bf16[192,2048]{1,0:T(8,128)(2,1)} %hid_ref.3, bf16[192,2048]{1,0:T(8,128)(2,1)} %get-tuple-element.9.xn_ref, f32[8,16,256]{2,1,0:T(8,128)} %get-tuple-element.10.rg_ref, s32[1,512]{1,0:T(1,128)} %get-tuple-element.11.back_ref, bf16[8,384,1408]{2,1,0:T(8,128)(2,1)} %get-tuple-element.12.h_ref, ...), custom_call_target="tpu_custom_call" | custom-call | tf_op jit(solution)/shard_map/down_sum/pallas_call | solution.py:609
  152.3 2.1 %copy.12 = bf16[192,2048]{1,0:T(8,128)(2,1)} copy(bf16[192,2048]{1,0:T(8,128)(2,1)} %down_sum.1) | data formatting | bytes 1572864

commit v5 on v4

--- a/solution.py
+++ b/solution.py
@@ -53,7 +53,7 @@
 def gather_up_kernel(
     n_kc, hid_ref, gain_ref, rw_ref, ids_ref, wg_ref, wu_ref, h_ref, rg_ref, xn_ref, tab_ref, back_ref,
     xall, pick, xsrc, acc, wbuf, hbuf, xe, meta_s, meta_r, ids_r, tab_v, tab_s,
-    sid, cid, ids_t, w_sem, h_sem, t_sem, x_sem, i_send, i_recv, m_send, m_recv, a_send, a_recv,
+    cid, ids_t, w_sem, h_sem, t_sem, x_sem, i_send, i_recv, m_send, m_recv, a_send, a_recv,
 ):
     me, core, x, y, sib, xnb, ynb = place()
     tok, dim = hid_ref.shape
@@ -114,8 +114,8 @@
 
     diag = me + 6 - 4 * x - 8 * y
     kinds = (
-        (me, sib, None), (me, xnb, None), (me, ynb, None), (xnb, ynb, 0), (ynb, xnb, 1),
-        (xnb, sib, None), (ynb, sib, None), (diag, sib, 0), (diag, sib, 1),
+        (me, sib, None), (me, xnb, 0), (me, ynb, 1), (xnb, ynb, 0), (ynb, xnb, 1),
+        (xnb, sib, None), (ynb, sib, None), (diag, sib, 0), (diag, sib, 1), (me, xnb, 1), (me, ynb, 0),
     )
 
     def copy(kc, kind):
@@ -132,8 +132,10 @@
 
     def serve_a(kc):
         received(kc, (1, 2))
-        start(kc, (3, 4, 5, 6))
-        pl.when(kc + 1 < n_kc)(lambda: start(kc + 1, (1, 2, 0)))
+        start(kc, (3, 4))
+        received(kc, (9, 10))
+        start(kc, (5, 6))
+        pl.when(kc + 1 < n_kc)(lambda: start(kc + 1, (1, 2, 9, 10, 0)))
 
     def serve_b(kc):
         received(kc, (3, 4))
@@ -148,7 +150,7 @@
 
     for k in range(1, 8):
         ids_copy(k).start()
-    start(0, (1, 2, 0))
+    start(0, (1, 2, 9, 10, 0))
     ids_r[pl.ds(my_pos, 1)] = ids_t[...].reshape(1, 8, 256)
 
     parts = lax.dot_general(
@@ -204,7 +206,6 @@
 
     for s in range(8):
         slot_id = jnp.where(masks[s], cums[s] - 1.0 + shift[:, s : s + 1], -1.0)
-        sid[s] = slot_id
         by_col = jnp.full((8, 256), -1.0, F32)
         for e in range(n_exp):
             by_col = jnp.where(ids_r[s] == me * n_exp + e, slot_id[e : e + 1], by_col)
@@ -312,8 +313,11 @@
     for k in range(1, 8):
         meta(k).wait_recv()
     for s in range(8):
-        rg_ref[s, :n_exp] = sid[s]
-        rg_ref[s, n_exp:] = meta_r[s]
+        gate_by_col = jnp.zeros((8, 256), F32)
+        for e in range(n_exp):
+            gate_by_col = jnp.where(ids_r[s] == me * n_exp + e, meta_r[s, e : e + 1, :], gate_by_col)
+        rg_ref[s, :8] = cid[s]
+        rg_ref[s, 8:] = gate_by_col
     for kc in range(n_kc):
         xn_copy(kc).wait()
     for k in range(1, 8):
@@ -325,13 +329,13 @@
 
 
 def down_kernel(
-    n_chunk, hid_ref, xn_ref, rg_ref, back_ref, h_ref, wd_ref, wsg_ref, wsu_ref, wsd_ref, out_ref,
-    hv, weigh, wdb, etile, esrc, part, got0, mid, got1, quart, got2, total, wsb, wdsb, hs,
+    n_chunk, rg_ref, back_ref, hid_hbm, xn_hbm, h_ref, wd_ref, wsg_ref, wsu_ref, wsd_ref, out_ref,
+    hv, weigh, wdb, etile, esrc, part, got0, mid, got1, quart, got2, total, wsb, wdsb, hs, xn_ref, hid_ref, x_sem,
     hv_sem, wd_sem, ws_sem, wds_sem, d_send, d_recv, p_send, p_recv, q_send, q_recv,
 ):
     me, core, x, y, sib, xnb, ynb = place()
     n_exp, cap, inter = h_ref.shape
-    tok, dim = hid_ref.shape
+    tok, dim = xn_hbm.shape
     n_et = cap // TILE
     n_slot = weigh.shape[-1]
     n_st = n_slot // TILE
@@ -384,23 +388,21 @@
         start(ws_copies(jnp.int32(i)))
     for i in range(2):
         wds_copy(jnp.int32(i)).start()
+    pltpu.make_async_copy(xn_hbm, xn_ref, x_sem.at[0]).start()
+    pltpu.make_async_copy(hid_hbm, hid_ref, x_sem.at[1]).start()
 
     barrier = pltpu.get_barrier_semaphore()
     for dev in (sib, xnb, ynb):
         pl.semaphore_signal(barrier, inc=1, device_id={"ep": dev}, device_id_type=pl.DeviceIdType.MESH)
 
-    def build(s, carry):
+    def build(s):
         slot = iota((tok, n_slot), 1).astype(F32)
         val = jnp.zeros((tok, n_slot), F32)
-        cols = jnp.concatenate([rg_ref[s], jnp.zeros((128 - 2 * n_exp, 256), F32)], axis=0).T[:tok]
-        for e in range(n_exp):
-            val = jnp.where(cols[:, e : e + 1] == slot, cols[:, n_exp + e : n_exp + e + 1], val)
+        cols = jnp.concatenate([rg_ref[s], jnp.zeros((112, 256), F32)], axis=0).T[:tok]
+        for k in range(6):
+            val = jnp.where(cols[:, k : k + 1] == slot, cols[:, 8 + k : 9 + k], val)
         for k, piece in enumerate(split3(val)):
             weigh[s, k * tok : (k + 1) * tok, :] = piece
-        return carry
-
-    lax.fori_loop(0, 8, build, 0)
-    pl.semaphore_wait(barrier, 3)
 
     def d_copy(n):
         b = lax.rem(n, 2)
@@ -453,30 +455,37 @@
             def _():
                 wd_copy(i).start()
 
+        for u in range(unroll):
+            wd_copy(i0 + u).wait()
+
+        def products():
+            for u in range(unroll):
+                e = j * unroll + u
+                res = dot_f32(hv[e], wdb[lax.rem(i0 + u, slots)]).astype(BF16)
+                etile[pl.ds(e * n_et, n_et)] = res.reshape(n_et, TILE, cw)
+
         @pl.when(n == 0)
         def _():
             for u in range(unroll):
                 h_copy(j * unroll + u).wait()
-
-        for u in range(unroll):
-            wd_copy(i0 + u).wait()
-        for u in range(unroll):
-            e = j * unroll + u
-            res = dot_f32(hv[e], wdb[lax.rem(i0 + u, slots)]).astype(BF16)
-            etile[pl.ds(e * n_et, n_et)] = res.reshape(n_et, TILE, cw)
+            products()
+            for u in range(8 // n_down):
+                build(j * (8 // n_down) + u)
+
+        pl.when(n > 0)(products)
 
     def combine(n, g):
         b = lax.rem(n, 2)
         for u in range(per_src):
-            s = g * per_src + u
+            s = (g + 1 - core - 2 * g * (1 - core)) * per_src + u
             for t in range(n_st):
                 esrc[u, t * TILE : (t + 1) * TILE, :] = etile[back_ref[0, s * 64 + t]]
         for u in range(per_src):
-            s = g * per_src + u
+            s = (g + 1 - core - 2 * g * (1 - core)) * per_src + u
             res = dot_f32(weigh[s], esrc[u])
             res = res[:tok] + (res[tok : 2 * tok] + res[2 * tok :])
             for hf in range(2):
-                part[b, hf, s // 4, pl.ds(pl.multiple_of(lax.rem(s, 4) * tok, tok), tok), :] = res[:, hf * hw : (hf + 1) * hw]
+                part[b, hf, s // 4, u * tok : (u + 1) * tok, :] = res[:, hf * hw : (hf + 1) * hw]
 
     def shared_up(i):
         ahead = i + wsb.shape[0] - 1
@@ -493,9 +502,12 @@
         n, j = s // per_chunk, lax.rem(s, per_chunk)
         pl.when(j < n_down)(lambda: down(n, j))
         pl.when(j >= n_down)(lambda: combine(n, j - n_down))
-        pl.when(j == per_chunk - 1)(lambda: d_copy(n).start())
-
-        @pl.when(j == 1)
+        @pl.when(j == n_down)
+        def _():
+            pl.when(n == 0)(lambda: pl.semaphore_wait(barrier, 3))
+            d_copy(n).start()
+
+        @pl.when(j == 0)
         def _():
             pl.when(n >= 1)(lambda: stage_p(n - 1))
             pl.when(n >= 4)(lambda: stage_f(n - 4))
@@ -510,7 +522,7 @@
 
     def up_step(i, carry):
         shared_up(i)
-        pl.when(i == 1)(lambda: stage_p(last))
+        pl.when(i == 0)(lambda: stage_p(last))
         pl.when(i == 4)(lambda: stage_q(last - 1))
 
         @pl.when(i == 8)
@@ -520,6 +532,8 @@
 
         return carry
 
+    pltpu.make_async_copy(xn_hbm, xn_ref, x_sem.at[0]).wait()
+    pltpu.make_async_copy(hid_hbm, hid_ref, x_sem.at[1]).wait()
     lax.fori_loop(0, n_s, up_step, 0)
     for i in range(n_d):
         wds_copy(jnp.int32(i)).wait()
@@ -564,7 +578,7 @@
             functools.partial(gather_up_kernel, n_kc),
             out_shape=(
                 jax.ShapeDtypeStruct((n_exp, cap, inter), BF16),
-                jax.ShapeDtypeStruct((8, 2 * n_exp, 256), F32),
+                jax.ShapeDtypeStruct((8, 16, 256), F32),
                 jax.ShapeDtypeStruct((tok, dim), BF16),
                 jax.ShapeDtypeStruct((n_exp, 256), jnp.int32),
                 jax.ShapeDtypeStruct((1, 512), jnp.int32),
@@ -584,8 +598,7 @@
                 pltpu.VMEM((8, 8, 256), jnp.int32),
                 pltpu.VMEM((n_exp, 256), jnp.int32),
                 pltpu.SMEM((n_exp, 256), jnp.int32),
-                pltpu.VMEM((8, n_exp, 256), F32),
-                pltpu.VMEM((8, n_exp, 256), F32),
+                pltpu.VMEM((8, 8, 256), F32),
                 pltpu.VMEM((8, 256), jnp.int32),
                 dma((slots, 2)),
                 dma((2,)),
@@ -595,21 +608,21 @@
                 dma((8,)),
                 dma((8,)),
                 dma((8,)),
-                dma((n_kc, 9)),
-                dma((n_kc, 9)),
+                dma((n_kc, 11)),
+                dma((n_kc, 11)),
             ],
             compiler_params=pltpu.CompilerParams(collective_id=0, has_side_effects=True, vmem_limit_bytes=VMEM_LIMIT),
             name="gather_up",
         )(hidden_in, norm_gain.reshape(1, dim), router_w, expert_ids.T, w_gate, w_up)
 
-        n_chunk, dslots = 8, 8
+        n_chunk, dslots = 8, 12
         cw = dim // n_chunk
         hw = cw // 2
         sw, dw = 256, 512
         return pl.pallas_call(
             functools.partial(down_kernel, n_chunk),
             out_shape=jax.ShapeDtypeStruct((tok, dim), BF16),
-            in_specs=[vmem, vmem, vmem, smem, hbm, hbm, hbm, hbm, hbm],
+            in_specs=[vmem, smem, hbm, hbm, hbm, hbm, hbm, hbm, hbm],
             out_specs=vmem,
             scratch_shapes=[
                 pltpu.VMEM((n_exp, cap, inter), BF16),
@@ -627,6 +640,9 @@
                 pltpu.VMEM((5, dim, 2 * sw), BF16),
                 pltpu.VMEM((2, s_inter, dw), BF16),
                 pltpu.VMEM((s_inter // sw, tok, sw), BF16),
+                pltpu.VMEM((tok, dim), BF16),
+                pltpu.VMEM((tok, dim), BF16),
+                dma((2,)),
                 dma((n_exp,)),
                 dma((dslots,)),
                 dma((5, 2)),
@@ -640,7 +656,7 @@
             ],
             compiler_params=pltpu.CompilerParams(collective_id=1, has_side_effects=True, vmem_limit_bytes=VMEM_LIMIT),
             name="down_sum",
-        )(hidden_in, xn, rg, back, h, w_down, ws_gate, ws_up, ws_down)
+        )(rg, back, hidden_in, xn, h, w_down, ws_gate, ws_up, ws_down)
 
     row_spec = P(("dp", "ep"), None)
     in_specs = (row_spec, P(), P(), P("ep"), P("ep"), P("ep"), P(), P(), P(), row_spec)

time: 155 us -> 152 us (0.981)
  Pallas kernels: 152 us -> 149 us
where the time goes in v5:
time: 152 us
  Pallas kernels  149 us (98%)
  local copies, waits for them, and re-layouts  2.09 us (1%)
    pallas_call x1, Pallas kernels, local_block(): pl.pallas_call(functools.partial(gather_up_kernel, n_kc), out_shape=(jax....  77.3 us
    pallas_call x1, Pallas kernels, local_block(): pl.pallas_call(functools.partial(down_kernel, n_chunk), out_shape=jax.Sha...  72.2 us

profile of v5, /device:TPU:0, one launch (start us, length us, event | category | flops | bytes accessed | tf_op | source)
XLA Modules:
  0.0 151.5 jit_solution(17382845416612694112)
XLA Ops:
  0.0 77.3 %gather_up.1 = (bf16[8,384,1408]{2,1,0:T(8,128)(2,1)}, f32[8,16,256]{2,1,0:T(8,128)}, bf16[192,2048]{1,0:T(8,128)(2,1)}, s32[8,256]{1,0:T(8,128)}, s32[1,512]{1,0:T(1,128)}) custom-call(bf16[192,2048]{1,0:T(8,128)(2,1)} %hid_hbm.1, f32[1,2048]{1,0:T(1,128)} %bitcast.2, f32[64,2048]{1,0:T(8,128)} %rw_ref.1, s32[6,192]{1,0:T(8,128)} %bitcast.3, ...), custom_call_target="tpu_custom_call" | custom-call | tf_op jit(solution)/shard_map/gather_up/pallas_call | solution.py:577
  77.3 72.2 %down_sum.1 = bf16[192,2048]{1,0:T(8,128)(2,1)} custom-call(f32[8,16,256]{2,1,0:T(8,128)} %get-tuple-element.9.rg_ref, s32[1,512]{1,0:T(1,128)} %get-tuple-element.10.back_ref, bf16[192,2048]{1,0:T(8,128)(2,1)} %hid_hbm.1, bf16[192,2048]{1,0:T(8,128)(2,1)} %get-tuple-element.11.xn_hbm, bf16[8,384,1408]{2,1,0:T(8,128)(2,1)} %get-tuple-element.12.h_ref, ...), custom_call_target="tpu_custom_call" | custom-call | tf_op jit(solution)/shard_map/down_sum/pallas_call | solution.py:622
  149.4 2.1 %copy.12 = bf16[192,2048]{1,0:T(8,128)(2,1)} copy(bf16[192,2048]{1,0:T(8,128)(2,1)} %down_sum.1) | data formatting | bytes 1572864

commit v6 on v5

--- a/solution.py
+++ b/solution.py
@@ -384,12 +384,13 @@
         wd_copy(jnp.int32(i)).start()
     for e in range(1, n_exp):
         h_copy(e).start()
-    for i in range(wsb.shape[0] - 1):
-        start(ws_copies(jnp.int32(i)))
-    for i in range(2):
-        wds_copy(jnp.int32(i)).start()
-    pltpu.make_async_copy(xn_hbm, xn_ref, x_sem.at[0]).start()
-    pltpu.make_async_copy(hid_hbm, hid_ref, x_sem.at[1]).start()
+    def late_copies():
+        for i in range(wsb.shape[0] - 1):
+            start(ws_copies(jnp.int32(i)))
+        for i in range(2):
+            wds_copy(jnp.int32(i)).start()
+        pltpu.make_async_copy(xn_hbm, xn_ref, x_sem.at[0]).start()
+        pltpu.make_async_copy(hid_hbm, hid_ref, x_sem.at[1]).start()
 
     barrier = pltpu.get_barrier_semaphore()
     for dev in (sib, xnb, ynb):
@@ -502,6 +503,7 @@
         n, j = s // per_chunk, lax.rem(s, per_chunk)
         pl.when(j < n_down)(lambda: down(n, j))
         pl.when(j >= n_down)(lambda: combine(n, j - n_down))
+        pl.when((n == 1) & (j == n_down))(late_copies)
         @pl.when(j == n_down)
         def _():
             pl.when(n == 0)(lambda: pl.semaphore_wait(barrier, 3))

time: 152 us -> 149 us (0.980)
  Pallas kernels: 149 us -> 147 us
    pallas_call x1, Pallas kernels: 72.2 us -> 69.9 us  [local_block(): pl.pallas_call(functools.partial(down_kernel, n_chunk), out_shape=jax.Sha...]
where the time goes in v6:
time: 149 us
  Pallas kernels  147 us (99%)
  local copies, waits for them, and re-layouts  2.09 us (1%)
    pallas_call x1, Pallas kernels, local_block(): pl.pallas_call(functools.partial(gather_up_kernel, n_kc), out_shape=(jax....  77.3 us
    pallas_call x1, Pallas kernels, local_block(): pl.pallas_call(functools.partial(down_kernel, n_chunk), out_shape=jax.Sha...  69.9 us

profile of v6, /device:TPU:0, one launch (start us, length us, event | category | flops | bytes accessed | tf_op | source)
XLA Modules:
  0.0 149.2 jit_solution(3303393306784390461)
XLA Ops:
  0.0 77.3 %gather_up.1 = (bf16[8,384,1408]{2,1,0:T(8,128)(2,1)}, f32[8,16,256]{2,1,0:T(8,128)}, bf16[192,2048]{1,0:T(8,128)(2,1)}, s32[8,256]{1,0:T(8,128)}, s32[1,512]{1,0:T(1,128)}) custom-call(bf16[192,2048]{1,0:T(8,128)(2,1)} %hid_hbm.1, f32[1,2048]{1,0:T(1,128)} %bitcast.2, f32[64,2048]{1,0:T(8,128)} %rw_ref.1, s32[6,192]{1,0:T(8,128)} %bitcast.3, ...), custom_call_target="tpu_custom_call" | custom-call | tf_op jit(solution)/shard_map/gather_up/pallas_call | solution.py:579
  77.3 69.9 %down_sum.1 = bf16[192,2048]{1,0:T(8,128)(2,1)} custom-call(f32[8,16,256]{2,1,0:T(8,128)} %get-tuple-element.9.rg_ref, s32[1,512]{1,0:T(1,128)} %get-tuple-element.10.back_ref, bf16[192,2048]{1,0:T(8,128)(2,1)} %hid_hbm.1, bf16[192,2048]{1,0:T(8,128)(2,1)} %get-tuple-element.11.xn_hbm, bf16[8,384,1408]{2,1,0:T(8,128)(2,1)} %get-tuple-element.12.h_ref, ...), custom_call_target="tpu_custom_call" | custom-call | tf_op jit(solution)/shard_map/down_sum/pallas_call | solution.py:624
  147.1 2.1 %copy.12 = bf16[192,2048]{1,0:T(8,128)(2,1)} copy(bf16[192,2048]{1,0:T(8,128)(2,1)} %down_sum.1) | data formatting | bytes 1572864
